TPU v7x, 128 devices: a whole 4x4x4 slice. The times are simulated.
128 devices in a mesh: tensor: 4 (over z_hi, core), dp: 32 (over y, x, z_lo).
Axes of the slice: x: 4, y: 4, z: 4 (z_hi: 2, z_lo: 2; z = z_hi * 2 + z_lo), core: 2. Of those that a mesh axis runs over, the one named last changes fastest.
Arguments:
- grads: bfloat16 [32, 4, 8192, 1024], P('dp', None, None, 'tensor'), may hold values from -6 to 6
- param: float32 [4, 8192, 1024], P(None, 'dp', 'tensor'), may hold values from -3 to 3
- q_m: bfloat16 [4, 8192, 1024], P(None, 'dp', 'tensor'), may hold values from -1 to 1
- m_scale: float32 [4], replicated, may hold values from 0.02 to 0.2
- q_v: bfloat16 [4, 8192, 1024], P(None, 'dp', 'tensor'), may hold values from 0.0009994507 to 1
- v_max: float32 [4, 8], P(None, 'tensor'), may hold values from 0.005 to 0.05
- v_exp: float32 [4, 8], P(None, 'tensor'), may hold values from 1 to 10
Outputs:
- new_param: float32 [4, 8192, 1024], P(None, 'dp', 'tensor')
- new_q_m: bfloat16 [4, 8192, 1024], P(None, 'dp', 'tensor')
- new_m_scale: float32 [4], replicated
- new_q_v: bfloat16 [4, 8192, 1024], P(None, 'dp', 'tensor')
- new_v_max: float32 [4, 8], P(None, 'tensor')
- new_v_exp: float32 [4, 8], P(None, 'tensor')
All inputs are finite; a program needn't handle non-finite values. Where the computation divides by a largest or mean magnitude, that divisor is 1e-20 or more.
Results may differ from a plain program's by a relative error of at most 0.001.
Values sent between devices are 32-bit elements; how exact they have to be, the bound alone decides.
A program may use at most 192 MiB of HBM per device.

v0:
```python
import jax
import jax.numpy as jnp
from jax import lax
from jax.sharding import Mesh
from jax.sharding import PartitionSpec as P

DP = ("dp_0", "dp_1", "dp_2")


def from_everyone(value, axis):
    copies = jnp.broadcast_to(value, (lax.axis_size(axis), *value.shape))
    return lax.all_to_all(copies, axis, split_axis=0, concat_axis=0, tiled=True)


def over_copies(value, axis):
    everything = from_everyone(value, axis)
    return jnp.max(everything, axis=0)


def packed_total(arrays, axis):
    flat, at, done = (jnp.concatenate([a.reshape(-1) for a in arrays]), 0, [])
    running = over_copies(flat, axis)
    for a in arrays:
        done.append(running[at : at + a.size].reshape(a.shape))
        at += a.size
    return tuple(done)


def split_up(value, dim, length):
    before, after = (value.shape[:dim], value.shape[dim + 1 :])
    return jnp.moveaxis(value.reshape(*before, length, -1, *after), dim, 0)


def cut_rows(length, count):
    unit = 8 if length >= 8 * count else 1
    return [length // unit * k // count * unit for k in range(1, count)]


def sum_in_order(pieces, axes, sequence):
    lengths = [lax.axis_size(a) for a in axes]
    pieces = pieces.reshape(*lengths, *pieces.shape[1:])
    pieces = pieces.transpose(*sequence, *range(len(axes), pieces.ndim))
    pieces = pieces.reshape(-1, *pieces.shape[len(axes) :])
    for k in sequence:
        pieces = lax.psum_scatter(pieces, axes[k], scatter_dimension=0, tiled=True)
    return pieces[0]


def spread_scatter(value, axes, dim):
    pieces = split_up(value, dim, lax.axis_size(axes))
    split_at = max(range(1, max(2, pieces.ndim - 1)), key=lambda d: pieces.shape[d])
    count, done = (len(axes), [])
    for first, piece in enumerate(
        jnp.split(pieces, cut_rows(pieces.shape[split_at], count), axis=split_at)
    ):
        if piece.size:
            sequence = [(first + k) % count for k in range(count)]
            done.append(sum_in_order(piece, axes, sequence))
    return jnp.concatenate(done, axis=split_at - 1)


def extremes(local_peak, local_top, local_low):
    row_top, group_top, group_neg = packed_total((local_peak, local_top, -local_low), DP)
    whole_top = over_copies(row_top, "tensor")
    return (whole_top, group_top, -group_neg)


def advance(summed, param, q_m, m_scale, q_v, v_max, v_exp, replicas):
    count, rows, width = q_m.shape
    groups = v_max.shape[1]
    shape4 = (count, rows, groups, width // groups)
    grad = (summed / replicas).reshape(shape4)
    m_old = m_scale[:, None, None, None] * q_m.astype(jnp.float32).reshape(shape4)
    stored = q_v.astype(jnp.float32).reshape(shape4)
    v_old = v_max[:, None, :, None] * jnp.exp(jnp.log(stored) / v_exp[:, None, :, None])
    m_new = 0.9 * m_old + 0.1 * grad
    v_new = 0.95 * v_old + 0.05 * grad * grad
    weights = param.reshape(shape4)
    new_param = weights - 0.02 * (m_new / (jnp.sqrt(v_new) + 1e-08) + 0.1 * weights)
    local_peak = jnp.max(jnp.abs(m_new), axis=(1, 2, 3))
    local_top = jnp.max(v_new, axis=(1, 3))
    local_low = jnp.min(v_new, axis=(1, 3))
    whole_top, group_top, group_low = extremes(local_peak, local_top, local_low)
    new_m_scale = whole_top + 1e-06
    new_v_exp = 12.343 / jnp.maximum(jnp.log(group_top / group_low), 1.0)
    new_q_m = (m_new / new_m_scale[:, None, None, None]).astype(jnp.bfloat16)
    new_q_v = jnp.exp(
        new_v_exp[:, None, :, None] * jnp.log(v_new / group_top[:, None, :, None])
    ).astype(jnp.bfloat16)
    flat = (count, rows, width)
    return (
        new_param.reshape(flat),
        new_q_m.reshape(flat),
        new_m_scale,
        new_q_v.reshape(flat),
        group_top,
        new_v_exp,
    )


def on_device(grads, param, q_m, m_scale, q_v, v_max, v_exp):
    replicas = lax.axis_size(DP)
    local = grads[0]
    summed = spread_scatter(local.astype(jnp.float32), DP, 1)
    return advance(summed, param, q_m, m_scale, q_v, v_max, v_exp, replicas)


def solution(mesh):
    split = Mesh(
        mesh.devices.reshape(mesh.shape["tensor"], 4, 4, 2), ("tensor", "dp_0", "dp_1", "dp_2")
    )
    return jax.shard_map(
        on_device,
        mesh=split,
        in_specs=(
            P(DP, None, None, "tensor"),
            P(None, DP, "tensor"),
            P(None, DP, "tensor"),
            P(),
            P(None, DP, "tensor"),
            P(None, "tensor"),
            P(None, "tensor"),
        ),
        out_specs=(
            P(None, DP, "tensor"),
            P(None, DP, "tensor"),
            P(),
            P(None, DP, "tensor"),
            P(None, "tensor"),
            P(None, "tensor"),
        ),
        check_vma=False,
    )
```

profile of v0, /device:TPU:1, one launch (start us, length us, event | category | flops | bytes accessed | tf_op | source)
XLA Modules:
  0.0 708.7 jit_solution(1104122156021086289)
XLA Ops:
  7.2 18.6 %convert_bitcast_fusion = f32[32,4,256,256]{3,2,0,1:T(8,128)} fusion(bf16[4,32,256,256]{3,2,1,0:T(8,128)(2,1)} %bitcast.69), kind=kLoop, calls=%fused_computation | loop fusion | flops 8388608 | bytes 50331648 | tf_op jit(solution)/shard_map/transpose | solution.py:31
  25.8 4.0 slice-done
  29.8 5.0 copy.59
  34.8 13.9 %copy.69 = f32[4,8,320,256]{3,1,2,0:T(8,128)} copy(f32[4,8,320,256]{3,2,1,0:T(8,128)} %bitcast.68) | data formatting | bytes 20971520
  48.7 0.0 reduce-scatter.15.cloned.1.call-start
  48.7 17.5 %fusion.1 = (f32[32,4,88,256]{3,2,0,1:T(8,128)}, f32[32,4,88,256]{3,2,0,1:T(8,128)}) fusion(f32[32,4,256,256]{3,2,0,1:T(8,128)} %convert_bitcast_fusion), kind=kLoop, calls=%fused_computation.25 | loop fusion | bytes 46137344 | tf_op jit(solution)/shard_map/split | solution.py:54
  66.2 10.4 %copy.49 = f32[4,2,4,4,88,256]{5,4,3,2,1,0:T(8,128)} copy(f32[4,2,4,4,88,256]{5,4,1,0,2,3:T(8,128)} %bitcast.66) | data formatting | bytes 23068672 | tf_op jit(solution)/shard_map/transpose | solution.py:42
  76.6 0.0 reduce-scatter.21.cloned.1.call-start
  76.6 10.3 %copy.50 = f32[2,4,4,4,88,256]{5,4,3,2,1,0:T(8,128)} copy(f32[2,4,4,4,88,256]{5,4,0,2,1,3:T(8,128)} %bitcast.65) | data formatting | bytes 23068672 | tf_op jit(solution)/shard_map/transpose | solution.py:42
  87.0 0.0 all-reduce.5.cloned.1.call-start
  87.1 62.4 %reduce-scatter.27.cloned.1.call-done = f32[8,81920]{1,0:T(8,128)} async-done(((f32[32,81920]{1,0:T(8,128)}), f32[8,81920]{1,0:T(8,128)}) %reduce-scatter.27.cloned.1.call-update) | async-done | bytes 2621456
  149.5 4.1 copy.60
  153.7 0.0 reduce-scatter.17.cloned.1.call-start
  153.7 104.0 %reduce-scatter.15.cloned.1.call-done = f32[8,4,88,256]{3,2,1,0:T(8,128)} async-done(((f32[32,4,88,256]{3,2,1,0:T(8,128)}), f32[8,4,88,256]{3,2,1,0:T(8,128)}) %reduce-scatter.15.cloned.1.call-update) | async-done | bytes 2883600 | tf_op jit(solution)/shard_map/reduce_scatter | solution.py:45
  257.7 137.9 %reduce-scatter.21.cloned.1.call-done = f32[16,4,88,256]{3,2,1,0:T(8,128)} async-done(((f32[32,4,88,256]{3,2,1,0:T(8,128)}), f32[16,4,88,256]{3,2,1,0:T(8,128)}) %reduce-scatter.21.cloned.1.call-update) | async-done | bytes 5767184 | tf_op jit(solution)/shard_map/reduce_scatter | solution.py:45
  395.7 0.6 dynamic-slice
  396.9 69.0 %all-reduce.5.cloned.1.call-done = f32[8,4,80,256]{3,2,0,1:T(8,128)} async-done(((f32[8,4,80,256]{3,2,0,1:T(8,128)}), f32[8,4,80,256]{3,2,0,1:T(8,128)}) %all-reduce.5.cloned.1.call-update) | async-done | bytes 2621456
  466.0 2.0 constant_dynamic-slice_fusion
  468.0 43.2 %reduce-scatter.17.cloned.1.call-done = f32[4,4,88,256]{3,2,1,0:T(8,128)} async-done(((f32[8,4,88,256]{3,2,1,0:T(8,128)}), f32[4,4,88,256]{3,2,1,0:T(8,128)}) %reduce-scatter.17.cloned.1.call-update) | async-done | bytes 1441808 | tf_op jit(solution)/shard_map/reduce_scatter | solution.py:45
  511.2 0.2 reduce-scatter.25.cloned.1.call-start
  511.4 62.8 %reduce-scatter.23.cloned.1.call-done = f32[4,4,88,256]{3,2,1,0:T(8,128)} async-done(((f32[16,4,88,256]{3,2,1,0:T(8,128)}), f32[4,4,88,256]{3,2,1,0:T(8,128)}) %reduce-scatter.23.cloned.1.call-update) | async-done | bytes 1441808 | tf_op jit(solution)/shard_map/reduce_scatter | solution.py:45
  574.3 0.6 dynamic-slice.2
  574.9 0.1 copy.52
  575.0 0.1 broadcast_bitcast_fusion.2
  575.1 0.1 copy.51
  575.2 0.1 broadcast_bitcast_fusion.3
  575.2 39.9 %all-reduce.7.cloned.1.call-done = f32[2,4,80,256]{3,2,0,1:T(8,128)} async-done(((f32[2,4,80,256]{3,2,0,1:T(8,128)}), f32[2,4,80,256]{3,2,0,1:T(8,128)}) %all-reduce.7.cloned.1.call-update) | async-done | bytes 655376
  615.2 1.6 dynamic-slice_bitcast_fusion
  616.8 25.7 %reduce-scatter.19.cloned.1.call-done = f32[1,4,88,256]{3,2,1,0:T(8,128)} async-done(((f32[4,4,88,256]{3,2,1,0:T(8,128)}), f32[1,4,88,256]{3,2,1,0:T(8,128)}) %reduce-scatter.19.cloned.1.call-update) | async-done | bytes 360464 | tf_op jit(solution)/shard_map/reduce_scatter | solution.py:45
  642.5 27.1 %reduce-scatter.25.cloned.1.call-done = f32[1,4,88,256]{3,2,1,0:T(8,128)} async-done(((f32[4,4,88,256]{3,2,1,0:T(8,128)}), f32[1,4,88,256]{3,2,1,0:T(8,128)}) %reduce-scatter.25.cloned.1.call-update) | async-done | bytes 360464 | tf_op jit(solution)/shard_map/reduce_scatter | solution.py:45
  669.7 1.9 fusion
  671.6 0.1 bitcast_reduce_fusion
  671.7 0.1 copy.54
  671.7 0.1 neg.18
  671.8 0.1 copy.53
  671.9 0.1 reshape.156
  672.0 0.1 pad_maximum_fusion.1
  672.1 13.7 %all_to_all.12 = f32[32,1,20]{2,1,0:T(1,128)S(1)} all-to-all(f32[32,1,20]{2,1,0:T(1,128)S(1)} %broadcast_in_dim.4), channel_id=1, replica_groups=mesh['tensor'=4,'dp_0'=4,'dp_1'=4,'dp_2'=2] {'dp_0','dp_1','dp_2'}, dimensions={0} | all-to-all | bytes 5120 | tf_op jit(solution)/shard_map/all_to_all | solution.py:12
  685.8 0.1 reduce_max.47
  685.8 0.1 slice_negate_fusion
  685.9 0.1 reshape.157
  686.0 0.1 neg.20
  686.1 0.1 broadcast_bitcast_fusion
  686.2 0.1 broadcast_bitcast_fusion.1
  686.2 0.7 copy.58
  686.9 0.6 copy.57
  687.6 11.4 %all_to_all.13 = f32[4,1,4]{2,1,0:T(1,128)S(1)} all-to-all(f32[4,1,4]{2,1,0:T(1,128)S(1)} %broadcast_in_dim.5), channel_id=1, replica_groups=mesh['tensor'=4,'dp_0'=4,'dp_1'=4,'dp_2'=2] {'tensor'}, dimensions={0} | all-to-all | bytes 128 | tf_op jit(solution)/shard_map/all_to_all | solution.py:12
  699.0 3.1 divide_convert_fusion
  (42 shorter events, 0.4 us)
Async XLA Ops:
  7.2 142.3 %reduce-scatter.27.cloned.1.call-start = ((), (), s32[]{:S(2)}) async-start(), calls=%async_computation.15 | async-start | bytes 13107200
  25.8 4.0 slice-start
  48.7 209.0 %reduce-scatter.15.cloned.1.call-start = ((), (), s32[]{:S(2)}) async-start(), calls=%async_computation.9 | async-start | bytes 14417920 | tf_op jit(solution)/shard_map/reduce_scatter | solution.py:45
  76.6 319.0 %reduce-scatter.21.cloned.1.call-start = ((), (), s32[]{:S(2)}) async-start(), calls=%async_computation.12 | async-start | bytes 17301504 | tf_op jit(solution)/shard_map/reduce_scatter | solution.py:45
  86.9 308.8 %copy-start.8 = (u32[128]{0:T(128)S(1)}, u32[128]{0:T(128)}, u32[]{:S(2)}) copy-start(u32[128]{0:T(128)} %constant.38) | copy-start | bytes 1540
  86.9 487.4 %copy-start.7 = (u32[128]{0:T(128)S(1)}, u32[128]{0:T(128)}, u32[]{:S(2)}) copy-start(u32[128]{0:T(128)} %constant.42) | copy-start | bytes 1540
  86.9 488.0 %copy-start.4 = (f32[4,2]{0,1:T(2,128)S(1)}, f32[4,2]{0,1:T(2,128)}, u32[]{:S(2)}) copy-start(f32[4,2]{0,1:T(2,128)} %param.13) | copy-start | bytes 100
  87.0 488.1 %copy-start.5 = (f32[4,2]{0,1:T(2,128)S(1)}, f32[4,2]{0,1:T(2,128)}, u32[]{:S(2)}) copy-start(f32[4,2]{0,1:T(2,128)} %param.12) | copy-start | bytes 100
  87.0 582.7 %copy-start = (bf16[4,256,256]{2,1,0:T(8,128)(2,1)S(1)}, bf16[4,256,256]{2,1,0:T(8,128)(2,1)}, u32[]{:S(2)}) copy-start(bf16[4,256,256]{2,1,0:T(8,128)(2,1)} %param.9) | copy-start | bytes 1572868
  87.0 582.7 %copy-start.2 = (bf16[4,256,256]{2,1,0:T(8,128)(2,1)S(1)}, bf16[4,256,256]{2,1,0:T(8,128)(2,1)}, u32[]{:S(2)}) copy-start(bf16[4,256,256]{2,1,0:T(8,128)(2,1)} %param.11) | copy-start | bytes 1572868
  87.0 582.7 %copy-start.3 = (f32[4]{0:T(128)S(1)}, f32[4]{0:T(128)}, u32[]{:S(2)}) copy-start(f32[4]{0:T(128)} %param.10) | copy-start | bytes 52
  87.0 379.0 %all-reduce.5.cloned.1.call-start = ((), (), s32[]{:S(2)}) async-start(), calls=%async_computation.16 | async-start | bytes 5242880
  149.5 549.5 %copy-start.1 = (f32[4,256,256]{2,1,0:T(8,128)S(1)}, f32[4,256,256]{2,1,0:T(8,128)}, u32[]{:S(2)}) copy-start(f32[4,256,256]{2,1,0:T(8,128)} %param.8) | copy-start | bytes 3145732
  153.7 357.5 %reduce-scatter.17.cloned.1.call-start = ((), (), s32[]{:S(2)}) async-start(), calls=%async_computation.10 | async-start | bytes 4325376 | tf_op jit(solution)/shard_map/reduce_scatter | solution.py:45
  257.7 316.6 %reduce-scatter.23.cloned.1.call-start = ((), (), s32[]{:S(2)}) async-start(), calls=%async_computation.13 | async-start | bytes 7208960 | tf_op jit(solution)/shard_map/reduce_scatter | solution.py:45
  395.6 219.6 %all-reduce.7.cloned.1.call-start = ((), (), s32[]{:S(2)}) async-start(), calls=%async_computation.17 | async-start | bytes 1310720
  468.0 174.6 %reduce-scatter.19.cloned.1.call-start = ((), (), s32[]{:S(2)}) async-start(), calls=%async_computation.11 | async-start | bytes 1802240 | tf_op jit(solution)/shard_map/reduce_scatter | solution.py:45
  511.2 158.5 %reduce-scatter.25.cloned.1.call-start = ((), (), s32[]{:S(2)}) async-start(), calls=%async_computation.14 | async-start | bytes 1802240 | tf_op jit(solution)/shard_map/reduce_scatter | solution.py:45
  699.0 3.2 copy-start.6
Sparse Core Ops, SparseCore 0:
  48.8 100.6 reduce-scatter.26
  152.0 105.6 reduce-scatter.14
  260.1 135.4 reduce-scatter.20
  397.8 68.1 all-reduce.4
  468.2 42.9 reduce-scatter.16
  513.4 60.7 reduce-scatter.22
  577.3 37.8 all-reduce.6
  617.6 24.9 reduce-scatter.18
  645.0 24.6 reduce-scatter.24
where the time goes:
time: 709 us
  waiting for transfers between devices  572 us (81%)
  local copies, waits for them, and re-layouts  72.3 us (10%)
  blocking collectives  25.1 us (4%)
  other arithmetic  23.9 us (3%)
  between operations  14.6 us (2%)
    reduce_scatter x6, waiting for transfers between devices, sum_in_order(): pieces = lax.psum_scatter(pieces, axes[k], scatter_dimension=0, tiled=True)  401 us
    unnamed x12, waiting for transfers between devices  172 us
    unnamed x36, local copies, waits for them, and re-layouts  28 us
    all_to_all x2, blocking collectives, from_everyone(): return lax.all_to_all(copies, axis, split_axis=0, concat_axis=0, tiled=True)  25.1 us
    split x3, local copies, waits for them, and re-layouts, spread_scatter(): jnp.split(pieces, cut_rows(pieces.shape[split_at], count), axis=split_at)  21.4 us
    transpose x2, local copies, waits for them, and re-layouts, sum_in_order(): pieces = pieces.transpose(*sequence, *range(len(axes), pieces.ndim))  20.7 us
    transpose x1, other arithmetic, split_up(): return jnp.moveaxis(value.reshape(*before, length, -1, *after), dim, 0)  18.6 us
  transfers between devices with their start and end apart: 9, of which 9 were waited for; matrix products, arithmetic and copies ran while one was open for 7% of the time, Pallas kernels for 0%

commit v1 on v0

v1 whole, which is shorter than its diff:
```python
import jax
import jax.numpy as jnp
from jax import lax
from jax.experimental import pallas as pl
from jax.experimental.pallas import tpu as pltpu
from jax.sharding import Mesh
from jax.sharding import PartitionSpec as P

MESH = pl.DeviceIdType.MESH
DP = ("y", "x", "zl")
TENSOR = ("zh", "core")
ROWS = 256
LANES = 128
SPLIT = (64, 104, 88)
PARTS = ((0, 48), (48, 40))
N = 8
SEMS = 42
LIMIT = 55 * 2**20
ORDER = ("F1y", "F2z", "Z1a", "F2y", "S1", "A3z", "F1x", "F2x", "A1y", "A2y", "Z1b", "E", "A1x", "A2z", "A2x")
LAGS = dict(S1=0, A1y=2, A1x=1, Z1a=2, Z1b=2, F1y=5, F1x=2, A2z=2, A2y=6, A2x=3,
            F2z=4, F2y=8, F2x=6, A3z=6, E=10)


def columns(ref, m):
    t, g = lax.div(m, 2), lax.rem(m, 2)
    return ref.at[t, ..., pl.ds(pl.multiple_of(g * LANES, LANES), LANES)]


def kernel(
    g_hbm, p_hbm, qm_hbm, ms_ref, qv_hbm, vm_ref, ve_ref,
    par, mnew, lv, table,
    G, S0, X0, Y0, Z0, S1b, X1, Y1, Z1, S2, Z2, X2, Y2,
    qm, qv, grad, stat, wide, deep,
    rsem, ssem, gsem, psem, asem, atsem,
):
    y, x, z = lax.axis_index("y"), lax.axis_index("x"), lax.axis_index("zl")
    zh, core = lax.axis_index("zh"), lax.axis_index("core")

    lane = lax.broadcasted_iota(jnp.int32, (1, LANES), 1)

    def step_of(coord, d):
        return lax.rem(coord + (1 if d == 0 else 3), 4)

    def to(axis, d):
        if axis == "zl":
            return {"zl": 1 - z}
        return {axis: step_of(x if axis == "x" else y, d)}

    def remote(m, idx, src, dst, target):
        return pltpu.make_async_remote_copy(
            src_ref=src, dst_ref=dst, send_sem=ssem.at[m, idx], recv_sem=rsem.at[m, idx],
            device_id=target, device_id_type=MESH,
        )

    def load_g(m):
        return pltpu.make_async_copy(columns(g_hbm, m), G.at[m], gsem.at[m])

    def load_state(m):
        return [
            pltpu.make_async_copy(columns(h, m), v.at[m], psem.at[m, i])
            for i, (h, v) in enumerate(((p_hbm, par), (qm_hbm, qm), (qv_hbm, qv)))
        ]

    def local(kind, m, yy, xx, zz):
        if kind == 0:
            return G[m, yy, xx, zz, 0:64, :].astype(jnp.float32)
        if kind == 1:
            return G[m, yy, xx, zz, 64:176, :].astype(jnp.float32)[:104]
        return G[m, yy, xx, zz, 160:256, :].astype(jnp.float32)[8:]

    class Plane:
        def __init__(self, kind, first, second, p, q, stage, bx, by, bz):
            self.kind, self.first, self.second, self.p, self.q = kind, first, second, p, q
            self.stage, self.bx, self.by, self.bz, self.base = stage, bx, by, bz, 13 * kind

        def own(self, m, pp, qq, zz):
            yy, xx = (qq, pp) if self.kind == 0 else (pp, qq)
            return local(self.kind, m, yy, xx, zz)

        def far1(self, m, d):
            return remote(m, self.base + d, self.stage.at[lax.rem(m, 2), 0, d],
                          self.bx.at[m, 0, d], to(self.first, d))

        def own1(self, m, d):
            return remote(m, self.base + 2 + d, self.stage.at[lax.rem(m, 2), 1, d],
                          self.bx.at[m, 1, d], to(self.first, d))

        def acc1(self, m, d):
            return remote(m, self.base + 4 + d, self.bx.at[m, 0, d],
                          self.bx.at[m, 2, d], to(self.first, d))

        def far2(self, m, d):
            return remote(m, self.base + 6 + d, self.bx.at[m, 2, d, lax.rem(self.q + 2, 4)],
                          self.by.at[m, 0, d], to(self.second, d))

        def own2(self, m, d):
            return remote(m, self.base + 8 + d, self.bx.at[m, 2, 1 - d, step_of(self.q, d)],
                          self.by.at[m, 1, d], to(self.second, d))

        def acc2(self, m, d):
            return remote(m, self.base + 10 + d, self.by.at[m, 0, d],
                          self.by.at[m, 2, d], to(self.second, d))

        def last(self, m):
            return remote(m, self.base + 12, self.by.at[m, 2, 1 - z], self.bz.at[m], to("zl", 0))

        def S_far(self, m):
            slot = lax.rem(m, 2)
            for d in range(2):
                for q in range(4):
                    self.stage[slot, 0, d, q] = self.own(m, lax.rem(self.p + 2, 4), q, d)
                self.far1(m, d).start()

        def S_own(self, m):
            slot = lax.rem(m, 2)
            for d in range(2):
                for q in range(4):
                    self.stage[slot, 1, d, q] = self.own(m, step_of(self.p, d), q, 1 - d)
                self.own1(m, d).start()

        def A1(self, m):
            for d in range(2):
                self.far1(m, d).wait_recv()
                for q in range(4):
                    self.bx[m, 0, d, q] += self.own(m, step_of(self.p, d), q, d)
                self.acc1(m, d).start()

        def F1(self, m):
            for d in range(2):
                self.own1(m, d).wait_recv()
                self.acc1(m, d).wait_recv()
            for h in range(2):
                for q in range(4):
                    self.bx[m, 2, h, q] += self.own(m, self.p, q, h) + self.bx[m, 1, 1 - h, q]
            for d in range(2):
                self.far2(m, d).start()
            for d in range(2):
                self.own2(m, d).start()

        def A2(self, m):
            for d in range(2):
                self.far2(m, d).wait_recv()
                self.by[m, 0, d] += self.bx[m, 2, d, step_of(self.q, d)]
                self.acc2(m, d).start()

        def F2(self, m):
            for d in range(2):
                self.own2(m, d).wait_recv()
                self.acc2(m, d).wait_recv()
            for h in range(2):
                self.by[m, 2, h] += self.bx[m, 2, h, self.q] + self.by[m, 1, 1 - h]
            self.last(m).start()

        def total(self, m):
            self.last(m).wait_recv()
            return self.by[m, 2, z] + self.bz[m]

        def staged(self, m):
            return [f(m, d) for f in (self.far1, self.own1) for d in range(2)]

        def unstaged(self, m):
            return [
                f(m, d) for f in (self.acc1, self.far2, self.own2, self.acc2) for d in range(2)
            ] + [self.last(m)]

    class ZFirst:
        def xs(self, j):
            return lax.rem(x + (2, 1, 3, 0)[j], 4)

        def zsend(self, m, j):
            return remote(m, 26 + j, S2.at[lax.rem(m, 2), self.xs(j)], Z2.at[m, self.xs(j)],
                          to("zl", 0))

        def far1(self, m, d):
            return remote(m, 30 + d, Z2.at[m, self.xs(0), pl.ds(2 * d, 2)],
                          X2.at[m, 0, pl.ds(2 * d, 2)], to("x", d))

        def own1(self, m, d):
            return remote(m, 32 + d, Z2.at[m, self.xs(1 + d), pl.ds(2 - 2 * d, 2)],
                          X2.at[m, 1, pl.ds(2 - 2 * d, 2)], to("x", d))

        def acc1(self, m, d):
            return remote(m, 34 + d, X2.at[m, 0, pl.ds(2 * d, 2)], X2.at[m, 2, pl.ds(2 * d, 2)],
                          to("x", d))

        def far2(self, m, d):
            part = pl.ds(*PARTS[d])
            return remote(m, 36 + d, X2.at[m, 2, lax.rem(y + 2, 4), part], Y2.at[m, 0, part],
                          to("y", d))

        def own2(self, m, d):
            part = pl.ds(*PARTS[1 - d])
            return remote(m, 38 + d, X2.at[m, 2, step_of(y, d), part], Y2.at[m, 1, part],
                          to("y", d))

        def acc2(self, m, d):
            part = pl.ds(*PARTS[d])
            return remote(m, 40 + d, Y2.at[m, 0, part], Y2.at[m, 2, part], to("y", d))

        def S(self, m, js):
            slot = lax.rem(m, 2)
            for j in js:
                for yy in range(4):
                    S2[slot, self.xs(j), yy] = local(2, m, yy, self.xs(j), 1 - z)
                self.zsend(m, j).start()

        def Z(self, m, j):
            self.zsend(m, j).wait_recv()
            for yy in range(4):
                Z2[m, self.xs(j), yy] += local(2, m, yy, self.xs(j), z)

        def Z1a(self, m):
            self.Z(m, 0)
            for d in range(2):
                self.far1(m, d).start()
            self.Z(m, 1)
            self.own1(m, 0).start()

        def Z1b(self, m):
            self.Z(m, 2)
            self.own1(m, 1).start()
            self.Z(m, 3)

        def A1(self, m):
            for d in range(2):
                self.far1(m, d).wait_recv()
                for i in range(2):
                    X2[m, 0, 2 * d + i] += Z2[m, self.xs(1 + d), 2 * d + i]
                self.acc1(m, d).start()

        def F1(self, m):
            for d in range(2):
                self.own1(m, d).wait_recv()
                self.acc1(m, d).wait_recv()
            for yy in range(4):
                X2[m, 2, yy] += Z2[m, x, yy] + X2[m, 1, yy]
            for d in range(2):
                self.far2(m, d).start()
            for d in range(2):
                self.own2(m, d).start()

        def A2(self, m):
            for d in range(2):
                self.far2(m, d).wait_recv()
                part = pl.ds(*PARTS[d])
                Y2[m, 0, part] += X2[m, 2, step_of(y, d), part]
                self.acc2(m, d).start()

        def total(self, m):
            for d in range(2):
                self.own2(m, d).wait_recv()
                self.acc2(m, d).wait_recv()
            return X2[m, 2, y] + Y2[m, 1] + Y2[m, 2]

        def staged(self, m):
            return [self.zsend(m, j) for j in range(4)]

        def unstaged(self, m):
            return [
                f(m, d)
                for f in (self.far1, self.own1, self.acc1, self.far2, self.own2, self.acc2)
                for d in range(2)
            ]

    A = Plane(0, "x", "y", x, y, S0, X0, Y0, Z0)
    B = Plane(1, "y", "x", y, x, S1b, X1, Y1, Z1)
    C = ZFirst()

    def begin(m):
        @pl.when(m >= 2)
        def _():
            for c in A.staged(m - 2) + B.staged(m - 2) + C.staged(m - 2):
                c.wait_send()

        load_g(m).wait()

        @pl.when(m + 2 < N)
        def _():
            load_g(m + 2).start()

        for c in load_state(m):
            c.start()
        B.S_far(m)
        A.S_far(m)
        C.S(m, (0,))
        B.S_own(m)
        A.S_own(m)
        C.S(m, (1, 2, 3))

    def update(m):
        r0 = 0
        for color, s in zip((A, B, C), SPLIT):
            grad[r0 : r0 + s] = color.total(m)
            r0 += s
        for c in load_state(m):
            c.wait()
        t, g = lax.div(m, 2), lax.rem(m, 2)
        scale, top = ms_ref[t], vm_ref[g, t]
        inverse = 1.0 / jnp.full((8, LANES), ve_ref[g, t], jnp.float32)[0:1]
        rows = 32

        def body(i, carry):
            hi, lo, peak = carry
            at = pl.ds(pl.multiple_of(i * rows, rows), rows)
            gr = grad[at] * (1.0 / 32)
            m_old = scale * qm[m, at].astype(jnp.float32)
            v_old = top * jnp.exp(jnp.log(qv[m, at].astype(jnp.float32)) * inverse)
            m_new = 0.9 * m_old + 0.1 * gr
            v_new = 0.95 * v_old + 0.05 * gr * gr
            w = par[m, at]
            par[m, at] = w - 0.02 * (m_new / (jnp.sqrt(v_new) + 1e-8) + 0.1 * w)
            mnew[m, at] = m_new
            lv[m, at] = jnp.log(v_new)
            fold = lambda v: v.reshape(rows // 8, 8, LANES)
            return (
                jnp.maximum(hi, jnp.max(fold(v_new), axis=0)),
                jnp.minimum(lo, jnp.min(fold(v_new), axis=0)),
                jnp.maximum(peak, jnp.max(fold(jnp.abs(m_new)), axis=0)),
            )

        start = jnp.zeros((8, LANES), jnp.float32)
        hi, lo, peak = lax.fori_loop(0, ROWS // rows, body, (start, start + 3e38, start))
        row = stat[0:1]
        for i, v in enumerate((hi, -lo, peak)):
            v = jnp.max(jnp.max(v, axis=0, keepdims=True), axis=1, keepdims=True)
            row = jnp.where(lane == 8 * i + 4 * g + t, v, row)
        stat[0:1] = row
        for c in A.unstaged(m) + B.unstaged(m) + C.unstaged(m):
            c.wait_send()

    stat[...] = jnp.full(stat.shape, -3e38, jnp.float32)
    ops = dict(S1=begin, A1y=B.A1, A1x=A.A1, Z1a=C.Z1a, Z1b=C.Z1b, F1y=B.F1, F1x=A.F1,
               A2z=C.A1, A2y=B.A2, A2x=A.A2, F2z=C.F1, F2y=B.F2, F2x=A.F2, A3z=C.A2, E=update)

    flip = lambda v, b: v + b - 2 * b * v
    plane_peers = [
        {"y": lax.rem(y + j, 4), "x": lax.rem(x + k, 4)}
        for j in range(4) for k in range(4) if j or k
    ]
    column_peers = [
        {"zl": flip(z, i & 1), "core": flip(core, i >> 1 & 1), "zh": flip(zh, i >> 2)}
        for i in range(1, 8)
    ]

    load_g(0).start()
    barrier = pltpu.get_barrier_semaphore()
    peers = [to(axis, d) for axis in ("x", "y") for d in range(2)] + column_peers
    for peer in peers:
        pl.semaphore_signal(barrier, inc=1, device_id=peer, device_id_type=MESH)
    load_g(1).start()
    pl.semaphore_wait(barrier, len(peers))

    def step(k, _):
        for name in ORDER:
            m = k - LAGS[name]
            pl.when((m >= 0) & (m < N))(lambda f=ops[name], m=m: f(m))
        return 0

    lax.fori_loop(0, N + max(LAGS.values()), step, 0)

    first = 0
    for who, buf in ((plane_peers, wide), (column_peers, deep)):
        copies = [
            pltpu.make_async_remote_copy(
                src_ref=stat.at[pl.ds(8 * (first > 0), 1)], dst_ref=buf.at[pl.ds(i, 1)],
                send_sem=atsem.at[first + i], recv_sem=asem.at[first + i],
                device_id=peer, device_id_type=MESH,
            )
            for i, peer in enumerate(who)
        ]
        for c in copies:
            c.start()
        mine = stat[8:9] if first else stat[0:1]
        buf[len(who) : len(who) + 1] = mine
        for c in copies:
            c.wait_recv()
        most = jnp.max(buf[...], axis=0, keepdims=True)
        if first == 0:
            stat[8:9] = most
        else:
            table[...] = jnp.where(lane < 16, jnp.maximum(mine, buf[0:1]), most)
        for c in copies:
            c.wait_send()
        first += len(who)
    for m in (N - 2, N - 1):
        for c in A.staged(m) + B.staged(m) + C.staged(m):
            c.wait_send()


def finish(par, mnew, lv, table, np_hbm, nqm_hbm, nms_ref, nqv_hbm, nvm_ref, nve_ref, qmo, qvo, sem):
    def store_out(m, i):
        h, v = ((np_hbm, par), (nqm_hbm, qmo), (nqv_hbm, qvo))[i]
        return pltpu.make_async_copy(v.at[m], columns(h, m), sem.at[m, i])

    for m in range(N):
        store_out(m, 0).start()
    row = table[...]
    lane = lax.broadcasted_iota(jnp.int32, (1, LANES), 1)
    left = lambda v, k: pltpu.roll(v, LANES - k, 1)
    low, peak = -left(row, 8), left(row, 16)
    scale = jnp.maximum(peak, left(peak, 4)) + 1e-6
    new_exp = 12.343 / jnp.maximum(jnp.log(row / low), 1.0)
    log_top, inverse = jnp.log(row), 1.0 / scale
    pick = lambda v, i: jnp.max(jnp.where(lane == i, v, -3e38), axis=1, keepdims=True)
    for m in range(N):
        t, g = m // 2, m % 2
        qmo[m] = (mnew[m] * pick(inverse, t)).astype(jnp.bfloat16)
        store_out(m, 1).start()
        e, top = pick(new_exp, 4 * g + t), pick(log_top, 4 * g + t)
        qvo[m] = jnp.exp(e * (lv[m] - top)).astype(jnp.bfloat16)
        store_out(m, 2).start()
    nms_ref[...] = scale[:, 0:4]
    for g in range(2):
        nvm_ref[g : g + 1, :] = left(row, 4 * g)[:, 0:4] if g else row[:, 0:4]
        nve_ref[g : g + 1, :] = left(new_exp, 4 * g)[:, 0:4] if g else new_exp[:, 0:4]
    for m in range(N):
        for i in range(3):
            store_out(m, i).wait()


def on_device(grads, param, q_m, m_scale, q_v, v_max, v_exp):
    f32, bf16 = jnp.float32, jnp.bfloat16
    a, b, c = SPLIT
    plane = lambda s: [
        pltpu.VMEM((2, 2, 2, 4, s, LANES), f32),
        pltpu.VMEM((N, 3, 2, 4, s, LANES), f32),
        pltpu.VMEM((N, 3, 2, s, LANES), f32),
        pltpu.VMEM((N, s, LANES), f32),
    ]
    block = lambda kind: pltpu.VMEM((N, ROWS, LANES), kind)
    anywhere, smem = pl.BlockSpec(memory_space=pl.ANY), pl.BlockSpec(memory_space=pltpu.SMEM)
    vmem = pl.BlockSpec(memory_space=pltpu.VMEM)
    kept = pl.pallas_call(
        kernel,
        out_shape=(block(f32), block(f32), block(f32), pltpu.VMEM((1, LANES), f32)),
        in_specs=[anywhere, anywhere, anywhere, smem, anywhere, smem, smem],
        out_specs=(vmem,) * 4,
        scratch_shapes=[
            pltpu.VMEM((N, 4, 4, 2, ROWS, LANES), bf16),
            *plane(a),
            *plane(b),
            pltpu.VMEM((2, 4, 4, c, LANES), f32),
            pltpu.VMEM((N, 4, 4, c, LANES), f32),
            pltpu.VMEM((N, 3, 4, c, LANES), f32),
            pltpu.VMEM((N, 3, c, LANES), f32),
            block(bf16), block(bf16),
            pltpu.VMEM((ROWS, LANES), f32),
            pltpu.VMEM((16, LANES), f32),
            pltpu.VMEM((16, LANES), f32),
            pltpu.VMEM((8, LANES), f32),
            pltpu.SemaphoreType.DMA((N, SEMS)),
            pltpu.SemaphoreType.DMA((N, SEMS)),
            pltpu.SemaphoreType.DMA((N,)),
            pltpu.SemaphoreType.DMA((N, 3)),
            pltpu.SemaphoreType.DMA((22,)),
            pltpu.SemaphoreType.DMA((22,)),
        ],
        compiler_params=pltpu.CompilerParams(
            collective_id=0, has_side_effects=True, vmem_limit_bytes=LIMIT
        ),
    )(grads[0].reshape(4, 4, 4, 2, ROWS, 2 * LANES), param, q_m, m_scale, q_v, v_max.T, v_exp.T)
    small = lambda rows: jax.ShapeDtypeStruct((rows, 4), f32)
    new_param, new_q_m, ms, new_q_v, vm, ve = pl.pallas_call(
        finish,
        out_shape=(
            jax.ShapeDtypeStruct(param.shape, f32),
            jax.ShapeDtypeStruct(q_m.shape, bf16),
            small(1),
            jax.ShapeDtypeStruct(q_v.shape, bf16),
            small(2),
            small(2),
        ),
        in_specs=[vmem] * 4,
        out_specs=(anywhere, anywhere, vmem, anywhere, vmem, vmem),
        scratch_shapes=[block(bf16), block(bf16), pltpu.SemaphoreType.DMA((N, 3))],
        compiler_params=pltpu.CompilerParams(vmem_limit_bytes=8 * 2**20),
    )(*kept)
    return new_param, new_q_m, ms[0], new_q_v, vm.T, ve.T


def solution(mesh):
    split = Mesh(mesh.devices.reshape(2, 2, 4, 4, 2), TENSOR + DP)
    return jax.shard_map(
        on_device,
        mesh=split,
        in_specs=(
            P(DP, None, None, TENSOR),
            P(None, DP, TENSOR),
            P(None, DP, TENSOR),
            P(),
            P(None, DP, TENSOR),
            P(None, TENSOR),
            P(None, TENSOR),
        ),
        out_specs=(
            P(None, DP, TENSOR),
            P(None, DP, TENSOR),
            P(),
            P(None, DP, TENSOR),
            P(None, TENSOR),
            P(None, TENSOR),
        ),
        check_vma=False,
    )
```

time: 709 us -> 176 us (0.25)
  waiting for transfers between devices: 572 us -> 0 us
  Pallas kernels: 0 us -> 175 us
  local copies, waits for them, and re-layouts: 72.3 us -> 0 us
  blocking collectives: 25.1 us -> 0 us
  other arithmetic: 23.9 us -> 0 us
  between operations: 14.6 us -> 0.64 us
    reduce_scatter x6 -> x0, waiting for transfers between devices: 401 us -> none  [sum_in_order(): pieces = lax.psum_scatter(pieces, axes[k], scatter_dimension=0, tiled=True)]
    pallas_call x0 -> x2, Pallas kernels: none -> 175 us  [the longest x1 173 us: on_device(): pl.pallas_call(kernel, out_shape=(block(f32), block(f32), block(f32), plt...]
    unnamed x12 -> x0, waiting for transfers between devices: 172 us -> none
    unnamed x36 -> x0, local copies, waits for them, and re-layouts: 28 us -> none
    all_to_all x2 -> x0, blocking collectives: 25.1 us -> none  [from_everyone(): return lax.all_to_all(copies, axis, split_axis=0, concat_axis=0, tiled=True)]
    split x3 -> x0, local copies, waits for them, and re-layouts: 21.4 us -> none  [spread_scatter(): jnp.split(pieces, cut_rows(pieces.shape[split_at], count), axis=split_at)]
    transpose x2 -> x0, local copies, waits for them, and re-layouts: 20.7 us -> none  [sum_in_order(): pieces = pieces.transpose(*sequence, *range(len(axes), pieces.ndim))]
    transpose x1 -> x0, other arithmetic: 18.6 us -> none  [split_up(): return jnp.moveaxis(value.reshape(*before, length, -1, *after), dim, 0)]
  transfers between devices with their start and end apart: 9 -> 0, of which waited for: 9 -> 0; matrix products, arithmetic and copies ran while one was open for 7% -> 0% of each run, Pallas kernels for 0% -> 0%
where the time goes in v1:
time: 176 us
  Pallas kernels  175 us (99%)
    pallas_call x1, Pallas kernels, on_device(): pl.pallas_call(kernel, out_shape=(block(f32), block(f32), block(f32), plt...  173 us

profile of v1, /device:TPU:1, one launch (start us, length us, event | category | flops | bytes accessed | tf_op | source)
XLA Modules:
  0.0 175.9 jit_solution(14511030530170725093)
XLA Ops:
  0.6 173.2 %shard_map.118 = (f32[8,256,128]{2,1,0:T(8,128)S(1)}, f32[8,256,128]{2,1,0:T(8,128)S(1)}, f32[8,256,128]{2,1,0:T(8,128)S(1)}, f32[1,128]{1,0:T(1,128)S(1)}) custom-call(bf16[4,4,4,2,256,256]{5,4,3,2,1,0:T(8,128)(2,1)} %bitcast.6, f32[4,256,256]{2,1,0:T(8,128)} %p_hbm.1, bf16[4,256,256]{2,1,0:T(8,128)(2,1)} %qm_hbm.1, f32[4]{0:T(128)} %ms_ref.1, ...), custom_call_target="tpu_custom_call" | custom-call | tf_op jit(solution)/shard_map/pallas_call | solution.py:433
  173.9 2.1 %shard_map.119 = (f32[4,256,256]{2,1,0:T(8,128)}, bf16[4,256,256]{2,1,0:T(8,128)(2,1)}, f32[1,4]{1,0:T(1,128)}, bf16[4,256,256]{2,1,0:T(8,128)(2,1)}, f32[2,4]{1,0:T(2,128)}, /*index=5*/f32[2,4]{1,0:T(2,128)}) custom-call(f32[8,256,128]{2,1,0:T(8,128)S(1)} %get-tuple-element.16.par, f32[8,256,128]{2,1,0:T(8,128)S(1)} %get-tuple-element.17.mnew, ...), custom_call_target="tpu_custom_call" | custom-call | tf_op jit(solution)/shard_map/pallas_call | solution.py:463

commit v2 on v1

--- a/solution.py
+++ b/solution.py
@@ -16,9 +16,8 @@
 N = 8
 SEMS = 42
 LIMIT = 55 * 2**20
-ORDER = ("F1y", "F2z", "Z1a", "F2y", "S1", "A3z", "F1x", "F2x", "A1y", "A2y", "Z1b", "E", "A1x", "A2z", "A2x")
-LAGS = dict(S1=0, A1y=2, A1x=1, Z1a=2, Z1b=2, F1y=5, F1x=2, A2z=2, A2y=6, A2x=3,
-            F2z=4, F2y=8, F2x=6, A3z=6, E=10)
+ORDER = ('F2z', 'F2y', 'A2y', 'A1x', 'EA', 'F1x', 'Z1b', 'EC', 'S1', 'A1y', 'A2z', 'F2x', 'F1y', 'A2x', 'A3z', 'EB', 'Z1a')
+LAGS = {'S1': 0, 'A1y': 1, 'A1x': 2, 'Z1a': 2, 'Z1b': 3, 'F1y': 2, 'F1x': 3, 'A2z': 6, 'A2y': 4, 'A2x': 7, 'F2z': 15, 'F2y': 8, 'F2x': 16, 'A3z': 23, 'EA': 26, 'EB': 16, 'EC': 32}
 
 
 def columns(ref, m):
@@ -30,7 +29,7 @@
     g_hbm, p_hbm, qm_hbm, ms_ref, qv_hbm, vm_ref, ve_ref,
     par, mnew, lv, table,
     G, S0, X0, Y0, Z0, S1b, X1, Y1, Z1, S2, Z2, X2, Y2,
-    qm, qv, grad, stat, wide, deep,
+    qm, qv, stat, wide, deep,
     rsem, ssem, gsem, psem, asem, atsem,
 ):
     y, x, z = lax.axis_index("y"), lax.axis_index("x"), lax.axis_index("zl")
@@ -41,10 +40,16 @@
     def step_of(coord, d):
         return lax.rem(coord + (1 if d == 0 else 3), 4)
 
-    def to(axis, d):
-        if axis == "zl":
+    def place(m):
+        s = lax.rem(m, 2)
+        return x + s * (y - x), y + s * (x - y)
+
+    def to(m, axis, d):
+        if axis == "z":
             return {"zl": 1 - z}
-        return {axis: step_of(x if axis == "x" else y, d)}
+        s = lax.rem(m, 2)
+        s = s if axis == "u" else 1 - s
+        return {"x": x + (1 - s) * (step_of(x, d) - x), "y": y + s * (step_of(y, d) - y)}
 
     def remote(m, idx, src, dst, target):
         return pltpu.make_async_remote_copy(
@@ -61,7 +66,9 @@
             for i, (h, v) in enumerate(((p_hbm, par), (qm_hbm, qm), (qv_hbm, qv)))
         ]
 
-    def local(kind, m, yy, xx, zz):
+    def local(kind, m, uu, vv, zz):
+        s = lax.rem(m, 2)
+        yy, xx = vv + s * (uu - vv), uu + s * (vv - uu)
         if kind == 0:
             return G[m, yy, xx, zz, 0:64, :].astype(jnp.float32)
         if kind == 1:
@@ -69,91 +76,103 @@
         return G[m, yy, xx, zz, 160:256, :].astype(jnp.float32)[8:]
 
     class Plane:
-        def __init__(self, kind, first, second, p, q, stage, bx, by, bz):
-            self.kind, self.first, self.second, self.p, self.q = kind, first, second, p, q
+        def __init__(self, kind, first, second, stage, bx, by, bz):
+            self.kind, self.first, self.second = kind, first, second
             self.stage, self.bx, self.by, self.bz, self.base = stage, bx, by, bz, 13 * kind
 
         def own(self, m, pp, qq, zz):
-            yy, xx = (qq, pp) if self.kind == 0 else (pp, qq)
-            return local(self.kind, m, yy, xx, zz)
+            uu, vv = (pp, qq) if self.first == "u" else (qq, pp)
+            return local(self.kind, m, uu, vv, zz)
+
+        def at(self, m):
+            u, v = place(m)
+            return (u, v) if self.first == "u" else (v, u)
 
         def far1(self, m, d):
             return remote(m, self.base + d, self.stage.at[lax.rem(m, 2), 0, d],
-                          self.bx.at[m, 0, d], to(self.first, d))
+                          self.bx.at[m, 0, d], to(m, self.first, d))
 
         def own1(self, m, d):
             return remote(m, self.base + 2 + d, self.stage.at[lax.rem(m, 2), 1, d],
-                          self.bx.at[m, 1, d], to(self.first, d))
+                          self.bx.at[m, 1, d], to(m, self.first, d))
 
         def acc1(self, m, d):
             return remote(m, self.base + 4 + d, self.bx.at[m, 0, d],
-                          self.bx.at[m, 2, d], to(self.first, d))
+                          self.bx.at[m, 2, d], to(m, self.first, d))
 
         def far2(self, m, d):
-            return remote(m, self.base + 6 + d, self.bx.at[m, 2, d, lax.rem(self.q + 2, 4)],
-                          self.by.at[m, 0, d], to(self.second, d))
+            q = self.at(m)[1]
+            return remote(m, self.base + 6 + d, self.bx.at[m, 2, d, lax.rem(q + 2, 4)],
+                          self.by.at[m, 0, d], to(m, self.second, d))
 
         def own2(self, m, d):
-            return remote(m, self.base + 8 + d, self.bx.at[m, 2, 1 - d, step_of(self.q, d)],
-                          self.by.at[m, 1, d], to(self.second, d))
+            q = self.at(m)[1]
+            return remote(m, self.base + 8 + d, self.bx.at[m, 2, 1 - d, step_of(q, d)],
+                          self.by.at[m, 1, d], to(m, self.second, d))
 
         def acc2(self, m, d):
             return remote(m, self.base + 10 + d, self.by.at[m, 0, d],
-                          self.by.at[m, 2, d], to(self.second, d))
+                          self.by.at[m, 2, d], to(m, self.second, d))
 
         def last(self, m):
-            return remote(m, self.base + 12, self.by.at[m, 2, 1 - z], self.bz.at[m], to("zl", 0))
+            return remote(m, self.base + 12, self.by.at[m, 2, 1 - z], self.bz.at[m], to(m, "z", 0))
 
         def S_far(self, m):
-            slot = lax.rem(m, 2)
+            slot, p = lax.rem(m, 2), self.at(m)[0]
             for d in range(2):
                 for q in range(4):
-                    self.stage[slot, 0, d, q] = self.own(m, lax.rem(self.p + 2, 4), q, d)
+                    self.stage[slot, 0, d, q] = self.own(m, lax.rem(p + 2, 4), q, d)
                 self.far1(m, d).start()
 
         def S_own(self, m):
-            slot = lax.rem(m, 2)
+            slot, p = lax.rem(m, 2), self.at(m)[0]
             for d in range(2):
                 for q in range(4):
-                    self.stage[slot, 1, d, q] = self.own(m, step_of(self.p, d), q, 1 - d)
+                    self.stage[slot, 1, d, q] = self.own(m, step_of(p, d), q, 1 - d)
                 self.own1(m, d).start()
 
         def A1(self, m):
+            p = self.at(m)[0]
             for d in range(2):
                 self.far1(m, d).wait_recv()
                 for q in range(4):
-                    self.bx[m, 0, d, q] += self.own(m, step_of(self.p, d), q, d)
+                    self.bx[m, 0, d, q] += self.own(m, step_of(p, d), q, d)
                 self.acc1(m, d).start()
 
         def F1(self, m):
+            p = self.at(m)[0]
             for d in range(2):
                 self.own1(m, d).wait_recv()
                 self.acc1(m, d).wait_recv()
             for h in range(2):
                 for q in range(4):
-                    self.bx[m, 2, h, q] += self.own(m, self.p, q, h) + self.bx[m, 1, 1 - h, q]
+                    self.bx[m, 2, h, q] += self.own(m, p, q, h) + self.bx[m, 1, 1 - h, q]
             for d in range(2):
                 self.far2(m, d).start()
             for d in range(2):
                 self.own2(m, d).start()
 
         def A2(self, m):
+            q = self.at(m)[1]
             for d in range(2):
                 self.far2(m, d).wait_recv()
-                self.by[m, 0, d] += self.bx[m, 2, d, step_of(self.q, d)]
+                self.by[m, 0, d] += self.bx[m, 2, d, step_of(q, d)]
                 self.acc2(m, d).start()
 
         def F2(self, m):
+            q = self.at(m)[1]
             for d in range(2):
                 self.own2(m, d).wait_recv()
                 self.acc2(m, d).wait_recv()
             for h in range(2):
-                self.by[m, 2, h] += self.bx[m, 2, h, self.q] + self.by[m, 1, 1 - h]
+                self.by[m, 2, h] += self.bx[m, 2, h, q] + self.by[m, 1, 1 - h]
             self.last(m).start()
 
-        def total(self, m):
+        def arrive(self, m):
             self.last(m).wait_recv()
-            return self.by[m, 2, z] + self.bz[m]
+
+        def total(self, m, rows):
+            return self.by[m, 2, z, rows] + self.bz[m, rows]
 
         def staged(self, m):
             return [f(m, d) for f in (self.far1, self.own1) for d in range(2)]
@@ -164,50 +183,50 @@
             ] + [self.last(m)]
 
     class ZFirst:
-        def xs(self, j):
-            return lax.rem(x + (2, 1, 3, 0)[j], 4)
+        def us(self, m, j):
+            return lax.rem(place(m)[0] + (2, 1, 3, 0)[j], 4)
 
         def zsend(self, m, j):
-            return remote(m, 26 + j, S2.at[lax.rem(m, 2), self.xs(j)], Z2.at[m, self.xs(j)],
-                          to("zl", 0))
+            return remote(m, 26 + j, S2.at[lax.rem(m, 2), self.us(m, j)], Z2.at[m, self.us(m, j)],
+                          to(m, "z", 0))
 
         def far1(self, m, d):
-            return remote(m, 30 + d, Z2.at[m, self.xs(0), pl.ds(2 * d, 2)],
-                          X2.at[m, 0, pl.ds(2 * d, 2)], to("x", d))
+            return remote(m, 30 + d, Z2.at[m, self.us(m, 0), pl.ds(2 * d, 2)],
+                          X2.at[m, 0, pl.ds(2 * d, 2)], to(m, "u", d))
 
         def own1(self, m, d):
-            return remote(m, 32 + d, Z2.at[m, self.xs(1 + d), pl.ds(2 - 2 * d, 2)],
-                          X2.at[m, 1, pl.ds(2 - 2 * d, 2)], to("x", d))
+            return remote(m, 32 + d, Z2.at[m, self.us(m, 1 + d), pl.ds(2 - 2 * d, 2)],
+                          X2.at[m, 1, pl.ds(2 - 2 * d, 2)], to(m, "u", d))
 
         def acc1(self, m, d):
             return remote(m, 34 + d, X2.at[m, 0, pl.ds(2 * d, 2)], X2.at[m, 2, pl.ds(2 * d, 2)],
-                          to("x", d))
+                          to(m, "u", d))
 
         def far2(self, m, d):
             part = pl.ds(*PARTS[d])
-            return remote(m, 36 + d, X2.at[m, 2, lax.rem(y + 2, 4), part], Y2.at[m, 0, part],
-                          to("y", d))
+            return remote(m, 36 + d, X2.at[m, 2, lax.rem(place(m)[1] + 2, 4), part],
+                          Y2.at[m, 0, part], to(m, "v", d))
 
         def own2(self, m, d):
             part = pl.ds(*PARTS[1 - d])
-            return remote(m, 38 + d, X2.at[m, 2, step_of(y, d), part], Y2.at[m, 1, part],
-                          to("y", d))
+            return remote(m, 38 + d, X2.at[m, 2, step_of(place(m)[1], d), part],
+                          Y2.at[m, 1, part], to(m, "v", d))
 
         def acc2(self, m, d):
             part = pl.ds(*PARTS[d])
-            return remote(m, 40 + d, Y2.at[m, 0, part], Y2.at[m, 2, part], to("y", d))
+            return remote(m, 40 + d, Y2.at[m, 0, part], Y2.at[m, 2, part], to(m, "v", d))
 
         def S(self, m, js):
             slot = lax.rem(m, 2)
             for j in js:
-                for yy in range(4):
-                    S2[slot, self.xs(j), yy] = local(2, m, yy, self.xs(j), 1 - z)
+                for v in range(4):
+                    S2[slot, self.us(m, j), v] = local(2, m, self.us(m, j), v, 1 - z)
                 self.zsend(m, j).start()
 
         def Z(self, m, j):
             self.zsend(m, j).wait_recv()
-            for yy in range(4):
-                Z2[m, self.xs(j), yy] += local(2, m, yy, self.xs(j), z)
+            for v in range(4):
+                Z2[m, self.us(m, j), v] += local(2, m, self.us(m, j), v, z)
 
         def Z1a(self, m):
             self.Z(m, 0)
@@ -225,15 +244,15 @@
             for d in range(2):
                 self.far1(m, d).wait_recv()
                 for i in range(2):
-                    X2[m, 0, 2 * d + i] += Z2[m, self.xs(1 + d), 2 * d + i]
+                    X2[m, 0, 2 * d + i] += Z2[m, self.us(m, 1 + d), 2 * d + i]
                 self.acc1(m, d).start()
 
         def F1(self, m):
             for d in range(2):
                 self.own1(m, d).wait_recv()
                 self.acc1(m, d).wait_recv()
-            for yy in range(4):
-                X2[m, 2, yy] += Z2[m, x, yy] + X2[m, 1, yy]
+            for v in range(4):
+                X2[m, 2, v] += Z2[m, place(m)[0], v] + X2[m, 1, v]
             for d in range(2):
                 self.far2(m, d).start()
             for d in range(2):
@@ -243,14 +262,16 @@
             for d in range(2):
                 self.far2(m, d).wait_recv()
                 part = pl.ds(*PARTS[d])
-                Y2[m, 0, part] += X2[m, 2, step_of(y, d), part]
+                Y2[m, 0, part] += X2[m, 2, step_of(place(m)[1], d), part]
                 self.acc2(m, d).start()
 
-        def total(self, m):
+        def arrive(self, m):
             for d in range(2):
                 self.own2(m, d).wait_recv()
                 self.acc2(m, d).wait_recv()
-            return X2[m, 2, y] + Y2[m, 1] + Y2[m, 2]
+
+        def total(self, m, rows):
+            return X2[m, 2, place(m)[1], rows] + Y2[m, 1, rows] + Y2[m, 2, rows]
 
         def staged(self, m):
             return [self.zsend(m, j) for j in range(4)]
@@ -262,8 +283,8 @@
                 for d in range(2)
             ]
 
-    A = Plane(0, "x", "y", x, y, S0, X0, Y0, Z0)
-    B = Plane(1, "y", "x", y, x, S1b, X1, Y1, Z1)
+    A = Plane(0, "u", "v", S0, X0, Y0, Z0)
+    B = Plane(1, "v", "u", S1b, X1, Y1, Z1)
     C = ZFirst()
 
     def begin(m):
@@ -278,59 +299,68 @@
         def _():
             load_g(m + 2).start()
 
-        for c in load_state(m):
-            c.start()
         B.S_far(m)
         A.S_far(m)
         C.S(m, (0,))
         B.S_own(m)
         A.S_own(m)
         C.S(m, (1, 2, 3))
-
-    def update(m):
-        r0 = 0
-        for color, s in zip((A, B, C), SPLIT):
-            grad[r0 : r0 + s] = color.total(m)
-            r0 += s
         for c in load_state(m):
             c.wait()
+
+        @pl.when(m + 1 < N)
+        def _():
+            for c in load_state(m + 1):
+                c.start()
+
+    def update(m, color, r0, size):
+        color.arrive(m)
         t, g = lax.div(m, 2), lax.rem(m, 2)
         scale, top = ms_ref[t], vm_ref[g, t]
         inverse = 1.0 / jnp.full((8, LANES), ve_ref[g, t], jnp.float32)[0:1]
-        rows = 32
-
-        def body(i, carry):
-            hi, lo, peak = carry
-            at = pl.ds(pl.multiple_of(i * rows, rows), rows)
-            gr = grad[at] * (1.0 / 32)
-            m_old = scale * qm[m, at].astype(jnp.float32)
-            v_old = top * jnp.exp(jnp.log(qv[m, at].astype(jnp.float32)) * inverse)
+        hi = peak = jnp.zeros((8, LANES), jnp.float32)
+        lo = hi + 3e38
+        at = r0
+        while at < r0 + size:
+            base = at // 16 * 16
+            rows = min(base + 32 if base == at else base + 16, r0 + size) - at
+            here = pl.ds(at, rows)
+            half = lambda ref: ref[m, base : base + 32 if rows > 16 else base + 16].astype(
+                jnp.float32
+            )[at - base : at - base + rows]
+            gr = color.total(m, pl.ds(at - r0, rows)) * (1.0 / 32)
+            m_old = scale * half(qm)
+            v_old = top * jnp.exp(jnp.log(half(qv)) * inverse)
             m_new = 0.9 * m_old + 0.1 * gr
             v_new = 0.95 * v_old + 0.05 * gr * gr
-            w = par[m, at]
-            par[m, at] = w - 0.02 * (m_new / (jnp.sqrt(v_new) + 1e-8) + 0.1 * w)
-            mnew[m, at] = m_new
-            lv[m, at] = jnp.log(v_new)
+            w = par[m, here]
+            par[m, here] = w - 0.02 * (m_new / (jnp.sqrt(v_new) + 1e-8) + 0.1 * w)
+            mnew[m, here] = m_new
+            lv[m, here] = jnp.log(v_new)
             fold = lambda v: v.reshape(rows // 8, 8, LANES)
-            return (
-                jnp.maximum(hi, jnp.max(fold(v_new), axis=0)),
-                jnp.minimum(lo, jnp.min(fold(v_new), axis=0)),
-                jnp.maximum(peak, jnp.max(fold(jnp.abs(m_new)), axis=0)),
-            )
-
-        start = jnp.zeros((8, LANES), jnp.float32)
-        hi, lo, peak = lax.fori_loop(0, ROWS // rows, body, (start, start + 3e38, start))
+            hi = jnp.maximum(hi, jnp.max(fold(v_new), axis=0))
+            lo = jnp.minimum(lo, jnp.min(fold(v_new), axis=0))
+            peak = jnp.maximum(peak, jnp.max(fold(jnp.abs(m_new)), axis=0))
+            at += rows
         row = stat[0:1]
         for i, v in enumerate((hi, -lo, peak)):
             v = jnp.max(jnp.max(v, axis=0, keepdims=True), axis=1, keepdims=True)
-            row = jnp.where(lane == 8 * i + 4 * g + t, v, row)
+            row = jnp.where(lane == 8 * i + 4 * g + t, jnp.maximum(row, v), row)
         stat[0:1] = row
+
+    def drain(m):
         for c in A.unstaged(m) + B.unstaged(m) + C.unstaged(m):
             c.wait_send()
 
+    def update_c(m):
+        pl.when(m >= 1)(lambda: drain(m - 1))
+        update(m, C, 168, 88)
+
     stat[...] = jnp.full(stat.shape, -3e38, jnp.float32)
     ops = dict(S1=begin, A1y=B.A1, A1x=A.A1, Z1a=C.Z1a, Z1b=C.Z1b, F1y=B.F1, F1x=A.F1,
-               A2z=C.A1, A2y=B.A2, A2x=A.A2, F2z=C.F1, F2y=B.F2, F2x=A.F2, A3z=C.A2, E=update)
+               A2z=C.A1, A2y=B.A2, A2x=A.A2, F2z=C.F1, F2y=B.F2, F2x=A.F2, A3z=C.A2,
+               EA=lambda m: update(m, A, 0, 64), EB=lambda m: update(m, B, 64, 104), EC=update_c)
+    assert all(LAGS["EC"] + 1 > v for v in LAGS.values())
 
     flip = lambda v, b: v + b - 2 * b * v
     plane_peers = [
@@ -344,11 +374,13 @@
 
     load_g(0).start()
     barrier = pltpu.get_barrier_semaphore()
-    peers = [to(axis, d) for axis in ("x", "y") for d in range(2)] + column_peers
+    peers = [to(0, axis, d) for axis in ("u", "v") for d in range(2)] + column_peers
     for peer in peers:
         pl.semaphore_signal(barrier, inc=1, device_id=peer, device_id_type=MESH)
     load_g(1).start()
     pl.semaphore_wait(barrier, len(peers))
+    for c in load_state(0):
+        c.start()
 
     def step(k, _):
         for name in ORDER:
@@ -372,6 +404,11 @@
             c.start()
         mine = stat[8:9] if first else stat[0:1]
         buf[len(who) : len(who) + 1] = mine
+        if first == 0:
+            drain(N - 1)
+            for m in (N - 2, N - 1):
+                for c in A.staged(m) + B.staged(m) + C.staged(m):
+                    c.wait_send()
         for c in copies:
             c.wait_recv()
         most = jnp.max(buf[...], axis=0, keepdims=True)
@@ -382,9 +419,6 @@
         for c in copies:
             c.wait_send()
         first += len(who)
-    for m in (N - 2, N - 1):
-        for c in A.staged(m) + B.staged(m) + C.staged(m):
-            c.wait_send()
 
 
 def finish(par, mnew, lv, table, np_hbm, nqm_hbm, nms_ref, nqv_hbm, nvm_ref, nve_ref, qmo, qvo, sem):
@@ -444,7 +478,6 @@
             pltpu.VMEM((N, 3, 4, c, LANES), f32),
             pltpu.VMEM((N, 3, c, LANES), f32),
             block(bf16), block(bf16),
-            pltpu.VMEM((ROWS, LANES), f32),
             pltpu.VMEM((16, LANES), f32),
             pltpu.VMEM((16, LANES), f32),
             pltpu.VMEM((8, LANES), f32),

time: 176 us -> 170 us (0.966)
  Pallas kernels: 175 us -> 169 us
    pallas_call x1, Pallas kernels: 173 us -> 167 us  [on_device(): pl.pallas_call(kernel, out_shape=(block(f32), block(f32), block(f32), plt...]
where the time goes in v2:
time: 170 us; the launch traced here: 169 us
  Pallas kernels  169 us (99%)
    pallas_call x1, Pallas kernels, on_device(): pl.pallas_call(kernel, out_shape=(block(f32), block(f32), block(f32), plt...  167 us

profile of v2, /device:TPU:1, one launch (start us, length us, event | category | flops | bytes accessed | tf_op | source)
XLA Modules:
  0.0 169.5 jit_solution(7325609601724038135)
XLA Ops:
  0.6 166.8 %shard_map.118 = (f32[8,256,128]{2,1,0:T(8,128)S(1)}, f32[8,256,128]{2,1,0:T(8,128)S(1)}, f32[8,256,128]{2,1,0:T(8,128)S(1)}, f32[1,128]{1,0:T(1,128)S(1)}) custom-call(bf16[4,4,4,2,256,256]{5,4,3,2,1,0:T(8,128)(2,1)} %bitcast.6, f32[4,256,256]{2,1,0:T(8,128)} %p_hbm.1, bf16[4,256,256]{2,1,0:T(8,128)(2,1)} %qm_hbm.1, f32[4]{0:T(128)} %ms_ref.1, ...), custom_call_target="tpu_custom_call" | custom-call | tf_op jit(solution)/shard_map/pallas_call | solution.py:467
  167.4 2.1 %shard_map.119 = (f32[4,256,256]{2,1,0:T(8,128)}, bf16[4,256,256]{2,1,0:T(8,128)(2,1)}, f32[1,4]{1,0:T(1,128)}, bf16[4,256,256]{2,1,0:T(8,128)(2,1)}, f32[2,4]{1,0:T(2,128)}, /*index=5*/f32[2,4]{1,0:T(2,128)}) custom-call(f32[8,256,128]{2,1,0:T(8,128)S(1)} %get-tuple-element.16.par, f32[8,256,128]{2,1,0:T(8,128)S(1)} %get-tuple-element.17.mnew, ...), custom_call_target="tpu_custom_call" | custom-call | tf_op jit(solution)/shard_map/pallas_call | solution.py:496

commit v3 on v2

--- a/solution.py
+++ b/solution.py
@@ -13,11 +13,12 @@
 LANES = 128
 SPLIT = (64, 104, 88)
 PARTS = ((0, 48), (48, 40))
+LOADS = ((64, 112), (0, 64), (176, 80))
 N = 8
-SEMS = 42
+SEMS = 24
 LIMIT = 55 * 2**20
-ORDER = ('F2z', 'F2y', 'A2y', 'A1x', 'EA', 'F1x', 'Z1b', 'EC', 'S1', 'A1y', 'A2z', 'F2x', 'F1y', 'A2x', 'A3z', 'EB', 'Z1a')
-LAGS = {'S1': 0, 'A1y': 1, 'A1x': 2, 'Z1a': 2, 'Z1b': 3, 'F1y': 2, 'F1x': 3, 'A2z': 6, 'A2y': 4, 'A2x': 7, 'F2z': 15, 'F2y': 8, 'F2x': 16, 'A3z': 23, 'EA': 26, 'EB': 16, 'EC': 32}
+ORDER = ('A1y', 'A2z', 'F2y', 'F2x', 'EC', 'EA', 'A1x', 'A3z', 'F2z', 'F1y', 'A2x', 'A2y', 'Z1a', 'F1x', 'Z1b', 'EB', 'S1')
+LAGS = {'S1': 0, 'A1y': 2, 'A1x': 2, 'Z1a': 3, 'Z1b': 4, 'F1y': 3, 'F1x': 3, 'A2z': 7, 'A2y': 4, 'A2x': 8, 'F2z': 20, 'F2y': 8, 'F2x': 22, 'A3z': 34, 'EA': 36, 'EB': 22, 'EC': 51}
 
 
 def columns(ref, m):
@@ -26,11 +27,11 @@
 
 
 def kernel(
-    g_hbm, p_hbm, qm_hbm, ms_ref, qv_hbm, vm_ref, ve_ref,
+    g_hbm, p_hbm, qm_hbm, ms_hbm, qv_hbm, vm_hbm, ve_hbm,
     par, mnew, lv, table,
     G, S0, X0, Y0, Z0, S1b, X1, Y1, Z1, S2, Z2, X2, Y2,
-    qm, qv, stat, wide, deep,
-    rsem, ssem, gsem, psem, asem, atsem,
+    qm, qv, stat, wide, deep, ms_ref, vm_ref, ve_ref,
+    rsem, ssem, stsem, gsem, psem, asem, atsem, csem,
 ):
     y, x, z = lax.axis_index("y"), lax.axis_index("x"), lax.axis_index("zl")
     zh, core = lax.axis_index("zh"), lax.axis_index("core")
@@ -51,18 +52,33 @@
         s = s if axis == "u" else 1 - s
         return {"x": x + (1 - s) * (step_of(x, d) - x), "y": y + s * (step_of(y, d) - y)}
 
-    def remote(m, idx, src, dst, target):
+    def remote(m, idx, src, dst, target, staged=None):
+        sent = ssem.at[m] if staged is None else stsem.at[lax.rem(m, 2), staged]
         return pltpu.make_async_remote_copy(
-            src_ref=src, dst_ref=dst, send_sem=ssem.at[m, idx], recv_sem=rsem.at[m, idx],
+            src_ref=src, dst_ref=dst, send_sem=sent, recv_sem=rsem.at[m, idx],
             device_id=target, device_id_type=MESH,
         )
 
-    def load_g(m):
-        return pltpu.make_async_copy(columns(g_hbm, m), G.at[m], gsem.at[m])
+    def arrived(m, idx, block):
+        remote(m, idx, block, block, to(m, "u", 0)).wait_recv()
+
+    def left(m, block, staged=None):
+        remote(m, 0, block, block, to(m, "u", 0), staged).wait_send()
+
+    def load_g(m, i):
+        rows = pl.ds(*LOADS[i])
+        return pltpu.make_async_copy(
+            columns(g_hbm, m).at[:, :, :, rows], G.at[m, :, :, :, rows], gsem.at[lax.rem(m, 2), i]
+        )
+
+    scalars = [
+        pltpu.make_async_copy(h, v, csem.at[i])
+        for i, (h, v) in enumerate(((ms_hbm, ms_ref), (vm_hbm, vm_ref), (ve_hbm, ve_ref)))
+    ]
 
     def load_state(m):
         return [
-            pltpu.make_async_copy(columns(h, m), v.at[m], psem.at[m, i])
+            pltpu.make_async_copy(columns(h, m), v.at[m], psem.at[i])
             for i, (h, v) in enumerate(((p_hbm, par), (qm_hbm, qm), (qv_hbm, qv)))
         ]
 
@@ -78,7 +94,7 @@
     class Plane:
         def __init__(self, kind, first, second, stage, bx, by, bz):
             self.kind, self.first, self.second = kind, first, second
-            self.stage, self.bx, self.by, self.bz, self.base = stage, bx, by, bz, 13 * kind
+            self.stage, self.bx, self.by, self.bz, self.base = stage, bx, by, bz, 7 * kind
 
         def own(self, m, pp, qq, zz):
             uu, vv = (pp, qq) if self.first == "u" else (qq, pp)
@@ -90,32 +106,32 @@
 
         def far1(self, m, d):
             return remote(m, self.base + d, self.stage.at[lax.rem(m, 2), 0, d],
-                          self.bx.at[m, 0, d], to(m, self.first, d))
+                          self.bx.at[m, 0, d], to(m, self.first, d), self.kind)
 
         def own1(self, m, d):
-            return remote(m, self.base + 2 + d, self.stage.at[lax.rem(m, 2), 1, d],
-                          self.bx.at[m, 1, d], to(m, self.first, d))
+            return remote(m, self.base + 2, self.stage.at[lax.rem(m, 2), 1, d],
+                          self.bx.at[m, 1, d], to(m, self.first, d), self.kind)
 
         def acc1(self, m, d):
-            return remote(m, self.base + 4 + d, self.bx.at[m, 0, d],
+            return remote(m, self.base + 2, self.bx.at[m, 0, d],
                           self.bx.at[m, 2, d], to(m, self.first, d))
 
         def far2(self, m, d):
             q = self.at(m)[1]
-            return remote(m, self.base + 6 + d, self.bx.at[m, 2, d, lax.rem(q + 2, 4)],
+            return remote(m, self.base + 3 + d, self.bx.at[m, 2, d, lax.rem(q + 2, 4)],
                           self.by.at[m, 0, d], to(m, self.second, d))
 
         def own2(self, m, d):
             q = self.at(m)[1]
-            return remote(m, self.base + 8 + d, self.bx.at[m, 2, 1 - d, step_of(q, d)],
+            return remote(m, self.base + 5, self.bx.at[m, 2, 1 - d, step_of(q, d)],
                           self.by.at[m, 1, d], to(m, self.second, d))
 
         def acc2(self, m, d):
-            return remote(m, self.base + 10 + d, self.by.at[m, 0, d],
+            return remote(m, self.base + 5, self.by.at[m, 0, d],
                           self.by.at[m, 2, d], to(m, self.second, d))
 
         def last(self, m):
-            return remote(m, self.base + 12, self.by.at[m, 2, 1 - z], self.bz.at[m], to(m, "z", 0))
+            return remote(m, self.base + 6, self.by.at[m, 2, 1 - z], self.bz.at[m], to(m, "z", 0))
 
         def S_far(self, m):
             slot, p = lax.rem(m, 2), self.at(m)[0]
@@ -141,9 +157,7 @@
 
         def F1(self, m):
             p = self.at(m)[0]
-            for d in range(2):
-                self.own1(m, d).wait_recv()
-                self.acc1(m, d).wait_recv()
+            arrived(m, self.base + 2, self.bx.at[m, pl.ds(1, 2)])
             for h in range(2):
                 for q in range(4):
                     self.bx[m, 2, h, q] += self.own(m, p, q, h) + self.bx[m, 1, 1 - h, q]
@@ -161,9 +175,7 @@
 
         def F2(self, m):
             q = self.at(m)[1]
-            for d in range(2):
-                self.own2(m, d).wait_recv()
-                self.acc2(m, d).wait_recv()
+            arrived(m, self.base + 5, self.by.at[m, pl.ds(1, 2)])
             for h in range(2):
                 self.by[m, 2, h] += self.bx[m, 2, h, q] + self.by[m, 1, 1 - h]
             self.last(m).start()
@@ -175,46 +187,41 @@
             return self.by[m, 2, z, rows] + self.bz[m, rows]
 
         def staged(self, m):
-            return [f(m, d) for f in (self.far1, self.own1) for d in range(2)]
-
-        def unstaged(self, m):
-            return [
-                f(m, d) for f in (self.acc1, self.far2, self.own2, self.acc2) for d in range(2)
-            ] + [self.last(m)]
+            left(m, self.stage.at[lax.rem(m, 2)], self.kind)
 
     class ZFirst:
         def us(self, m, j):
             return lax.rem(place(m)[0] + (2, 1, 3, 0)[j], 4)
 
         def zsend(self, m, j):
-            return remote(m, 26 + j, S2.at[lax.rem(m, 2), self.us(m, j)], Z2.at[m, self.us(m, j)],
-                          to(m, "z", 0))
+            return remote(m, 14 + j, S2.at[lax.rem(m, 2), self.us(m, j)], Z2.at[m, self.us(m, j)],
+                          to(m, "z", 0), 2)
 
         def far1(self, m, d):
-            return remote(m, 30 + d, Z2.at[m, self.us(m, 0), pl.ds(2 * d, 2)],
+            return remote(m, 18 + d, Z2.at[m, self.us(m, 0), pl.ds(2 * d, 2)],
                           X2.at[m, 0, pl.ds(2 * d, 2)], to(m, "u", d))
 
         def own1(self, m, d):
-            return remote(m, 32 + d, Z2.at[m, self.us(m, 1 + d), pl.ds(2 - 2 * d, 2)],
+            return remote(m, 20, Z2.at[m, self.us(m, 1 + d), pl.ds(2 - 2 * d, 2)],
                           X2.at[m, 1, pl.ds(2 - 2 * d, 2)], to(m, "u", d))
 
         def acc1(self, m, d):
-            return remote(m, 34 + d, X2.at[m, 0, pl.ds(2 * d, 2)], X2.at[m, 2, pl.ds(2 * d, 2)],
+            return remote(m, 20, X2.at[m, 0, pl.ds(2 * d, 2)], X2.at[m, 2, pl.ds(2 * d, 2)],
                           to(m, "u", d))
 
         def far2(self, m, d):
             part = pl.ds(*PARTS[d])
-            return remote(m, 36 + d, X2.at[m, 2, lax.rem(place(m)[1] + 2, 4), part],
+            return remote(m, 21 + d, X2.at[m, 2, lax.rem(place(m)[1] + 2, 4), part],
                           Y2.at[m, 0, part], to(m, "v", d))
 
         def own2(self, m, d):
             part = pl.ds(*PARTS[1 - d])
-            return remote(m, 38 + d, X2.at[m, 2, step_of(place(m)[1], d), part],
+            return remote(m, 23, X2.at[m, 2, step_of(place(m)[1], d), part],
                           Y2.at[m, 1, part], to(m, "v", d))
 
         def acc2(self, m, d):
             part = pl.ds(*PARTS[d])
-            return remote(m, 40 + d, Y2.at[m, 0, part], Y2.at[m, 2, part], to(m, "v", d))
+            return remote(m, 23, Y2.at[m, 0, part], Y2.at[m, 2, part], to(m, "v", d))
 
         def S(self, m, js):
             slot = lax.rem(m, 2)
@@ -248,9 +255,7 @@
                 self.acc1(m, d).start()
 
         def F1(self, m):
-            for d in range(2):
-                self.own1(m, d).wait_recv()
-                self.acc1(m, d).wait_recv()
+            arrived(m, 20, X2.at[m, pl.ds(1, 2)])
             for v in range(4):
                 X2[m, 2, v] += Z2[m, place(m)[0], v] + X2[m, 1, v]
             for d in range(2):
@@ -266,22 +271,13 @@
                 self.acc2(m, d).start()
 
         def arrive(self, m):
-            for d in range(2):
-                self.own2(m, d).wait_recv()
-                self.acc2(m, d).wait_recv()
+            arrived(m, 23, Y2.at[m, pl.ds(1, 2)])
 
         def total(self, m, rows):
             return X2[m, 2, place(m)[1], rows] + Y2[m, 1, rows] + Y2[m, 2, rows]
 
         def staged(self, m):
-            return [self.zsend(m, j) for j in range(4)]
-
-        def unstaged(self, m):
-            return [
-                f(m, d)
-                for f in (self.far1, self.own1, self.acc1, self.far2, self.own2, self.acc2)
-                for d in range(2)
-            ]
+            left(m, S2.at[lax.rem(m, 2)], 2)
 
     A = Plane(0, "u", "v", S0, X0, Y0, Z0)
     B = Plane(1, "v", "u", S1b, X1, Y1, Z1)
@@ -290,23 +286,31 @@
     def begin(m):
         @pl.when(m >= 2)
         def _():
-            for c in A.staged(m - 2) + B.staged(m - 2) + C.staged(m - 2):
-                c.wait_send()
-
-        load_g(m).wait()
+            for color in (A, B, C):
+                color.staged(m - 2)
+
+        load_g(m, 0).wait()
+        B.S_far(m)
+        load_g(m, 1).wait()
+        A.S_far(m)
+        load_g(m, 2).wait()
+        C.S(m, (0,))
 
         @pl.when(m + 2 < N)
         def _():
-            load_g(m + 2).start()
-
-        B.S_far(m)
-        A.S_far(m)
-        C.S(m, (0,))
+            for i in range(3):
+                load_g(m + 2, i).start()
+
         B.S_own(m)
         A.S_own(m)
         C.S(m, (1, 2, 3))
         for c in load_state(m):
             c.wait()
+
+        @pl.when(m == 0)
+        def _():
+            for c in scalars:
+                c.wait()
 
         @pl.when(m + 1 < N)
         def _():
@@ -349,8 +353,7 @@
         stat[0:1] = row
 
     def drain(m):
-        for c in A.unstaged(m) + B.unstaged(m) + C.unstaged(m):
-            c.wait_send()
+        left(m, G.at[m, :, :, :, pl.ds(0, 240)])
 
     def update_c(m):
         pl.when(m >= 1)(lambda: drain(m - 1))
@@ -365,21 +368,24 @@
     flip = lambda v, b: v + b - 2 * b * v
     plane_peers = [
         {"y": lax.rem(y + j, 4), "x": lax.rem(x + k, 4)}
-        for j in range(4) for k in range(4) if j or k
+        for j in (2, 1, 3, 0) for k in (2, 1, 3, 0) if j or k
     ]
     column_peers = [
         {"zl": flip(z, i & 1), "core": flip(core, i >> 1 & 1), "zh": flip(zh, i >> 2)}
         for i in range(1, 8)
     ]
 
-    load_g(0).start()
+    for i in range(3):
+        load_g(0, i).start()
     barrier = pltpu.get_barrier_semaphore()
-    peers = [to(0, axis, d) for axis in ("u", "v") for d in range(2)] + column_peers
+    peers = [to(0, axis, d) for axis in ("u", "v") for d in range(2)]
+    peers += [p for i, p in enumerate(column_peers, 1) if i not in (4, 6)]
     for peer in peers:
         pl.semaphore_signal(barrier, inc=1, device_id=peer, device_id_type=MESH)
-    load_g(1).start()
     pl.semaphore_wait(barrier, len(peers))
-    for c in load_state(0):
+    for i in range(3):
+        load_g(1, i).start()
+    for c in load_state(0) + scalars:
         c.start()
 
     def step(k, _):
@@ -390,35 +396,36 @@
 
     lax.fori_loop(0, N + max(LAGS.values()), step, 0)
 
-    first = 0
-    for who, buf in ((plane_peers, wide), (column_peers, deep)):
+    for phase, (who, buf) in enumerate(((plane_peers, wide), (column_peers, deep))):
         copies = [
             pltpu.make_async_remote_copy(
-                src_ref=stat.at[pl.ds(8 * (first > 0), 1)], dst_ref=buf.at[pl.ds(i, 1)],
-                send_sem=atsem.at[first + i], recv_sem=asem.at[first + i],
+                src_ref=stat.at[pl.ds(8 * phase, 1)], dst_ref=buf.at[pl.ds(i, 1)],
+                send_sem=atsem.at[phase], recv_sem=asem.at[phase],
                 device_id=peer, device_id_type=MESH,
             )
             for i, peer in enumerate(who)
         ]
         for c in copies:
             c.start()
-        mine = stat[8:9] if first else stat[0:1]
+        mine = stat[8 * phase : 8 * phase + 1]
         buf[len(who) : len(who) + 1] = mine
-        if first == 0:
+        if phase == 0:
             drain(N - 1)
             for m in (N - 2, N - 1):
-                for c in A.staged(m) + B.staged(m) + C.staged(m):
-                    c.wait_send()
-        for c in copies:
-            c.wait_recv()
+                for color in (A, B, C):
+                    color.staged(m)
+        everyone = pltpu.make_async_remote_copy(
+            src_ref=buf.at[pl.ds(0, len(who))], dst_ref=buf.at[pl.ds(0, len(who))],
+            send_sem=atsem.at[phase], recv_sem=asem.at[phase],
+            device_id=who[0], device_id_type=MESH,
+        )
+        everyone.wait_recv()
         most = jnp.max(buf[...], axis=0, keepdims=True)
-        if first == 0:
+        if phase == 0:
             stat[8:9] = most
         else:
             table[...] = jnp.where(lane < 16, jnp.maximum(mine, buf[0:1]), most)
-        for c in copies:
-            c.wait_send()
-        first += len(who)
+        everyone.wait_send()
 
 
 def finish(par, mnew, lv, table, np_hbm, nqm_hbm, nms_ref, nqv_hbm, nvm_ref, nve_ref, qmo, qvo, sem):
@@ -462,12 +469,12 @@
         pltpu.VMEM((N, s, LANES), f32),
     ]
     block = lambda kind: pltpu.VMEM((N, ROWS, LANES), kind)
-    anywhere, smem = pl.BlockSpec(memory_space=pl.ANY), pl.BlockSpec(memory_space=pltpu.SMEM)
+    anywhere = pl.BlockSpec(memory_space=pl.ANY)
     vmem = pl.BlockSpec(memory_space=pltpu.VMEM)
     kept = pl.pallas_call(
         kernel,
         out_shape=(block(f32), block(f32), block(f32), pltpu.VMEM((1, LANES), f32)),
-        in_specs=[anywhere, anywhere, anywhere, smem, anywhere, smem, smem],
+        in_specs=[anywhere] * 7,
         out_specs=(vmem,) * 4,
         scratch_shapes=[
             pltpu.VMEM((N, 4, 4, 2, ROWS, LANES), bf16),
@@ -481,12 +488,17 @@
             pltpu.VMEM((16, LANES), f32),
             pltpu.VMEM((16, LANES), f32),
             pltpu.VMEM((8, LANES), f32),
-            pltpu.SemaphoreType.DMA((N, SEMS)),
+            pltpu.SMEM((4,), f32),
+            pltpu.SMEM((2, 4), f32),
+            pltpu.SMEM((2, 4), f32),
             pltpu.SemaphoreType.DMA((N, SEMS)),
             pltpu.SemaphoreType.DMA((N,)),
-            pltpu.SemaphoreType.DMA((N, 3)),
-            pltpu.SemaphoreType.DMA((22,)),
-            pltpu.SemaphoreType.DMA((22,)),
+            pltpu.SemaphoreType.DMA((2, 3)),
+            pltpu.SemaphoreType.DMA((2, 3)),
+            pltpu.SemaphoreType.DMA((3,)),
+            pltpu.SemaphoreType.DMA((2,)),
+            pltpu.SemaphoreType.DMA((2,)),
+            pltpu.SemaphoreType.DMA((3,)),
         ],
         compiler_params=pltpu.CompilerParams(
             collective_id=0, has_side_effects=True, vmem_limit_bytes=LIMIT

time: 170 us -> 164 us (0.965)
  Pallas kernels: 169 us -> 163 us
    pallas_call x1, Pallas kernels: 167 us -> 161 us  [on_device(): pl.pallas_call(kernel, out_shape=(block(f32), block(f32), block(f32), plt...]
where the time goes in v3:
time: 164 us
  Pallas kernels  163 us (99%)
    pallas_call x1, Pallas kernels, on_device(): pl.pallas_call(kernel, out_shape=(block(f32), block(f32), block(f32), plt...  161 us

profile of v3, /device:TPU:1, one launch (start us, length us, event | category | flops | bytes accessed | tf_op | source)
XLA Modules:
  0.0 163.9 jit_solution(18221280725765791577)
XLA Ops:
  0.6 161.2 %shard_map.118 = (f32[8,256,128]{2,1,0:T(8,128)S(1)}, f32[8,256,128]{2,1,0:T(8,128)S(1)}, f32[8,256,128]{2,1,0:T(8,128)S(1)}, f32[1,128]{1,0:T(1,128)S(1)}) custom-call(bf16[4,4,4,2,256,256]{5,4,3,2,1,0:T(8,128)(2,1)} %bitcast.6, f32[4,256,256]{2,1,0:T(8,128)} %p_hbm.1, bf16[4,256,256]{2,1,0:T(8,128)(2,1)} %qm_hbm.1, f32[4]{0:T(128)} %ms_hbm.1, ...), custom_call_target="tpu_custom_call" | custom-call | tf_op jit(solution)/shard_map/pallas_call | solution.py:474
  161.8 2.1 %shard_map.119 = (f32[4,256,256]{2,1,0:T(8,128)}, bf16[4,256,256]{2,1,0:T(8,128)(2,1)}, f32[1,4]{1,0:T(1,128)}, bf16[4,256,256]{2,1,0:T(8,128)(2,1)}, f32[2,4]{1,0:T(2,128)}, /*index=5*/f32[2,4]{1,0:T(2,128)}) custom-call(f32[8,256,128]{2,1,0:T(8,128)S(1)} %get-tuple-element.16.par, f32[8,256,128]{2,1,0:T(8,128)S(1)} %get-tuple-element.17.mnew, ...), custom_call_target="tpu_custom_call" | custom-call | tf_op jit(solution)/shard_map/pallas_call | solution.py:508

commit v4 on v3

--- a/solution.py
+++ b/solution.py
@@ -15,7 +15,7 @@
 PARTS = ((0, 48), (48, 40))
 LOADS = ((64, 112), (0, 64), (176, 80))
 N = 8
-SEMS = 24
+SEMS = 16
 LIMIT = 55 * 2**20
 ORDER = ('A1y', 'A2z', 'F2y', 'F2x', 'EC', 'EA', 'A1x', 'A3z', 'F2z', 'F1y', 'A2x', 'A2y', 'Z1a', 'F1x', 'Z1b', 'EB', 'S1')
 LAGS = {'S1': 0, 'A1y': 2, 'A1x': 2, 'Z1a': 3, 'Z1b': 4, 'F1y': 3, 'F1x': 3, 'A2z': 7, 'A2y': 4, 'A2x': 8, 'F2z': 20, 'F2y': 8, 'F2x': 22, 'A3z': 34, 'EA': 36, 'EB': 22, 'EC': 51}
@@ -30,13 +30,11 @@
     g_hbm, p_hbm, qm_hbm, ms_hbm, qv_hbm, vm_hbm, ve_hbm,
     par, mnew, lv, table,
     G, S0, X0, Y0, Z0, S1b, X1, Y1, Z1, S2, Z2, X2, Y2,
-    qm, qv, stat, wide, deep, ms_ref, vm_ref, ve_ref,
+    qm, qv, most, stat, wide, deep, ms_ref, vm_ref, ve_ref,
     rsem, ssem, stsem, gsem, psem, asem, atsem, csem,
 ):
     y, x, z = lax.axis_index("y"), lax.axis_index("x"), lax.axis_index("zl")
     zh, core = lax.axis_index("zh"), lax.axis_index("core")
-
-    lane = lax.broadcasted_iota(jnp.int32, (1, LANES), 1)
 
     def step_of(coord, d):
         return lax.rem(coord + (1 if d == 0 else 3), 4)
@@ -94,7 +92,7 @@
     class Plane:
         def __init__(self, kind, first, second, stage, bx, by, bz):
             self.kind, self.first, self.second = kind, first, second
-            self.stage, self.bx, self.by, self.bz, self.base = stage, bx, by, bz, 7 * kind
+            self.stage, self.bx, self.by, self.bz, self.base = stage, bx, by, bz, 5 * kind
 
         def own(self, m, pp, qq, zz):
             uu, vv = (pp, qq) if self.first == "u" else (qq, pp)
@@ -105,33 +103,33 @@
             return (u, v) if self.first == "u" else (v, u)
 
         def far1(self, m, d):
-            return remote(m, self.base + d, self.stage.at[lax.rem(m, 2), 0, d],
+            return remote(m, self.base, self.stage.at[lax.rem(m, 2), 0, d],
                           self.bx.at[m, 0, d], to(m, self.first, d), self.kind)
 
         def own1(self, m, d):
-            return remote(m, self.base + 2, self.stage.at[lax.rem(m, 2), 1, d],
+            return remote(m, self.base + 1, self.stage.at[lax.rem(m, 2), 1, d],
                           self.bx.at[m, 1, d], to(m, self.first, d), self.kind)
 
         def acc1(self, m, d):
-            return remote(m, self.base + 2, self.bx.at[m, 0, d],
+            return remote(m, self.base + 1, self.bx.at[m, 0, d],
                           self.bx.at[m, 2, d], to(m, self.first, d))
 
         def far2(self, m, d):
             q = self.at(m)[1]
-            return remote(m, self.base + 3 + d, self.bx.at[m, 2, d, lax.rem(q + 2, 4)],
+            return remote(m, self.base + 2, self.bx.at[m, 2, d, lax.rem(q + 2, 4)],
                           self.by.at[m, 0, d], to(m, self.second, d))
 
         def own2(self, m, d):
             q = self.at(m)[1]
-            return remote(m, self.base + 5, self.bx.at[m, 2, 1 - d, step_of(q, d)],
+            return remote(m, self.base + 3, self.bx.at[m, 2, 1 - d, step_of(q, d)],
                           self.by.at[m, 1, d], to(m, self.second, d))
 
         def acc2(self, m, d):
-            return remote(m, self.base + 5, self.by.at[m, 0, d],
+            return remote(m, self.base + 3, self.by.at[m, 0, d],
                           self.by.at[m, 2, d], to(m, self.second, d))
 
         def last(self, m):
-            return remote(m, self.base + 6, self.by.at[m, 2, 1 - z], self.bz.at[m], to(m, "z", 0))
+            return remote(m, self.base + 4, self.by.at[m, 2, 1 - z], self.bz.at[m], to(m, "z", 0))
 
         def S_far(self, m):
             slot, p = lax.rem(m, 2), self.at(m)[0]
@@ -149,15 +147,15 @@
 
         def A1(self, m):
             p = self.at(m)[0]
-            for d in range(2):
-                self.far1(m, d).wait_recv()
+            arrived(m, self.base, self.bx.at[m, 0])
+            for d in range(2):
                 for q in range(4):
                     self.bx[m, 0, d, q] += self.own(m, step_of(p, d), q, d)
                 self.acc1(m, d).start()
 
         def F1(self, m):
             p = self.at(m)[0]
-            arrived(m, self.base + 2, self.bx.at[m, pl.ds(1, 2)])
+            arrived(m, self.base + 1, self.bx.at[m, pl.ds(1, 2)])
             for h in range(2):
                 for q in range(4):
                     self.bx[m, 2, h, q] += self.own(m, p, q, h) + self.bx[m, 1, 1 - h, q]
@@ -168,14 +166,14 @@
 
         def A2(self, m):
             q = self.at(m)[1]
-            for d in range(2):
-                self.far2(m, d).wait_recv()
+            arrived(m, self.base + 2, self.by.at[m, 0])
+            for d in range(2):
                 self.by[m, 0, d] += self.bx[m, 2, d, step_of(q, d)]
                 self.acc2(m, d).start()
 
         def F2(self, m):
             q = self.at(m)[1]
-            arrived(m, self.base + 5, self.by.at[m, pl.ds(1, 2)])
+            arrived(m, self.base + 3, self.by.at[m, pl.ds(1, 2)])
             for h in range(2):
                 self.by[m, 2, h] += self.bx[m, 2, h, q] + self.by[m, 1, 1 - h]
             self.last(m).start()
@@ -194,34 +192,34 @@
             return lax.rem(place(m)[0] + (2, 1, 3, 0)[j], 4)
 
         def zsend(self, m, j):
-            return remote(m, 14 + j, S2.at[lax.rem(m, 2), self.us(m, j)], Z2.at[m, self.us(m, j)],
+            return remote(m, 10 + j // 2, S2.at[lax.rem(m, 2), self.us(m, j)], Z2.at[m, self.us(m, j)],
                           to(m, "z", 0), 2)
 
         def far1(self, m, d):
-            return remote(m, 18 + d, Z2.at[m, self.us(m, 0), pl.ds(2 * d, 2)],
+            return remote(m, 12, Z2.at[m, self.us(m, 0), pl.ds(2 * d, 2)],
                           X2.at[m, 0, pl.ds(2 * d, 2)], to(m, "u", d))
 
         def own1(self, m, d):
-            return remote(m, 20, Z2.at[m, self.us(m, 1 + d), pl.ds(2 - 2 * d, 2)],
+            return remote(m, 13, Z2.at[m, self.us(m, 1 + d), pl.ds(2 - 2 * d, 2)],
                           X2.at[m, 1, pl.ds(2 - 2 * d, 2)], to(m, "u", d))
 
         def acc1(self, m, d):
-            return remote(m, 20, X2.at[m, 0, pl.ds(2 * d, 2)], X2.at[m, 2, pl.ds(2 * d, 2)],
+            return remote(m, 13, X2.at[m, 0, pl.ds(2 * d, 2)], X2.at[m, 2, pl.ds(2 * d, 2)],
                           to(m, "u", d))
 
         def far2(self, m, d):
             part = pl.ds(*PARTS[d])
-            return remote(m, 21 + d, X2.at[m, 2, lax.rem(place(m)[1] + 2, 4), part],
+            return remote(m, 14, X2.at[m, 2, lax.rem(place(m)[1] + 2, 4), part],
                           Y2.at[m, 0, part], to(m, "v", d))
 
         def own2(self, m, d):
             part = pl.ds(*PARTS[1 - d])
-            return remote(m, 23, X2.at[m, 2, step_of(place(m)[1], d), part],
+            return remote(m, 15, X2.at[m, 2, step_of(place(m)[1], d), part],
                           Y2.at[m, 1, part], to(m, "v", d))
 
         def acc2(self, m, d):
             part = pl.ds(*PARTS[d])
-            return remote(m, 23, Y2.at[m, 0, part], Y2.at[m, 2, part], to(m, "v", d))
+            return remote(m, 15, Y2.at[m, 0, part], Y2.at[m, 2, part], to(m, "v", d))
 
         def S(self, m, js):
             slot = lax.rem(m, 2)
@@ -231,11 +229,11 @@
                 self.zsend(m, j).start()
 
         def Z(self, m, j):
-            self.zsend(m, j).wait_recv()
             for v in range(4):
                 Z2[m, self.us(m, j), v] += local(2, m, self.us(m, j), v, z)
 
         def Z1a(self, m):
+            arrived(m, 10, Z2.at[m, pl.ds(0, 2)])
             self.Z(m, 0)
             for d in range(2):
                 self.far1(m, d).start()
@@ -243,19 +241,20 @@
             self.own1(m, 0).start()
 
         def Z1b(self, m):
+            arrived(m, 11, Z2.at[m, pl.ds(0, 2)])
             self.Z(m, 2)
             self.own1(m, 1).start()
             self.Z(m, 3)
 
         def A1(self, m):
-            for d in range(2):
-                self.far1(m, d).wait_recv()
+            arrived(m, 12, X2.at[m, 0])
+            for d in range(2):
                 for i in range(2):
                     X2[m, 0, 2 * d + i] += Z2[m, self.us(m, 1 + d), 2 * d + i]
                 self.acc1(m, d).start()
 
         def F1(self, m):
-            arrived(m, 20, X2.at[m, pl.ds(1, 2)])
+            arrived(m, 13, X2.at[m, pl.ds(1, 2)])
             for v in range(4):
                 X2[m, 2, v] += Z2[m, place(m)[0], v] + X2[m, 1, v]
             for d in range(2):
@@ -264,14 +263,14 @@
                 self.own2(m, d).start()
 
         def A2(self, m):
-            for d in range(2):
-                self.far2(m, d).wait_recv()
+            arrived(m, 14, Y2.at[m, 0])
+            for d in range(2):
                 part = pl.ds(*PARTS[d])
                 Y2[m, 0, part] += X2[m, 2, step_of(place(m)[1], d), part]
                 self.acc2(m, d).start()
 
         def arrive(self, m):
-            arrived(m, 23, Y2.at[m, pl.ds(1, 2)])
+            arrived(m, 15, Y2.at[m, pl.ds(1, 2)])
 
         def total(self, m, rows):
             return X2[m, 2, place(m)[1], rows] + Y2[m, 1, rows] + Y2[m, 2, rows]
@@ -346,11 +345,8 @@
             lo = jnp.minimum(lo, jnp.min(fold(v_new), axis=0))
             peak = jnp.maximum(peak, jnp.max(fold(jnp.abs(m_new)), axis=0))
             at += rows
-        row = stat[0:1]
         for i, v in enumerate((hi, -lo, peak)):
-            v = jnp.max(jnp.max(v, axis=0, keepdims=True), axis=1, keepdims=True)
-            row = jnp.where(lane == 8 * i + 4 * g + t, jnp.maximum(row, v), row)
-        stat[0:1] = row
+            most[i, m] = jnp.maximum(most[i, m], v)
 
     def drain(m):
         left(m, G.at[m, :, :, :, pl.ds(0, 240)])
@@ -359,7 +355,7 @@
         pl.when(m >= 1)(lambda: drain(m - 1))
         update(m, C, 168, 88)
 
-    stat[...] = jnp.full(stat.shape, -3e38, jnp.float32)
+    most[...] = jnp.full(most.shape, -3e38, jnp.float32)
     ops = dict(S1=begin, A1y=B.A1, A1x=A.A1, Z1a=C.Z1a, Z1b=C.Z1b, F1y=B.F1, F1x=A.F1,
                A2z=C.A1, A2y=B.A2, A2x=A.A2, F2z=C.F1, F2y=B.F2, F2x=A.F2, A3z=C.A2,
                EA=lambda m: update(m, A, 0, 64), EB=lambda m: update(m, B, 64, 104), EC=update_c)
@@ -372,14 +368,14 @@
     ]
     column_peers = [
         {"zl": flip(z, i & 1), "core": flip(core, i >> 1 & 1), "zh": flip(zh, i >> 2)}
-        for i in range(1, 8)
+        for i in range(7, 0, -1)
     ]
 
     for i in range(3):
         load_g(0, i).start()
     barrier = pltpu.get_barrier_semaphore()
     peers = [to(0, axis, d) for axis in ("u", "v") for d in range(2)]
-    peers += [p for i, p in enumerate(column_peers, 1) if i not in (4, 6)]
+    peers += [p for i, p in enumerate(column_peers) if i not in (1, 3)]
     for peer in peers:
         pl.semaphore_signal(barrier, inc=1, device_id=peer, device_id_type=MESH)
     pl.semaphore_wait(barrier, len(peers))
@@ -396,6 +392,14 @@
 
     lax.fori_loop(0, N + max(LAGS.values()), step, 0)
 
+    sub = lax.broadcasted_iota(jnp.int32, (N, LANES), 0)
+    lane = lax.broadcasted_iota(jnp.int32, (N, LANES), 1)
+    spread = jnp.full((N, LANES), -3e38, jnp.float32)
+    for i in range(3):
+        v = jnp.max(jnp.max(most[i], axis=1), axis=1, keepdims=True)
+        spread = jnp.where(lane == 8 * i + 4 * lax.rem(sub, 2) + lax.div(sub, 2), v, spread)
+    stat[0:1] = jnp.max(spread, axis=0, keepdims=True)
+    lane = lane[0:1]
     for phase, (who, buf) in enumerate(((plane_peers, wide), (column_peers, deep))):
         copies = [
             pltpu.make_async_remote_copy(
@@ -420,18 +424,18 @@
             device_id=who[0], device_id_type=MESH,
         )
         everyone.wait_recv()
-        most = jnp.max(buf[...], axis=0, keepdims=True)
+        top = jnp.max(buf[...], axis=0, keepdims=True)
         if phase == 0:
-            stat[8:9] = most
+            stat[8:9] = top
         else:
-            table[...] = jnp.where(lane < 16, jnp.maximum(mine, buf[0:1]), most)
+            table[...] = jnp.where(lane < 16, jnp.maximum(mine, buf[6:7]), top)
         everyone.wait_send()
 
 
 def finish(par, mnew, lv, table, np_hbm, nqm_hbm, nms_ref, nqv_hbm, nvm_ref, nve_ref, qmo, qvo, sem):
     def store_out(m, i):
         h, v = ((np_hbm, par), (nqm_hbm, qmo), (nqv_hbm, qvo))[i]
-        return pltpu.make_async_copy(v.at[m], columns(h, m), sem.at[m, i])
+        return pltpu.make_async_copy(v.at[m], columns(h, m), sem.at[i])
 
     for m in range(N):
         store_out(m, 0).start()
@@ -454,9 +458,8 @@
     for g in range(2):
         nvm_ref[g : g + 1, :] = left(row, 4 * g)[:, 0:4] if g else row[:, 0:4]
         nve_ref[g : g + 1, :] = left(new_exp, 4 * g)[:, 0:4] if g else new_exp[:, 0:4]
-    for m in range(N):
-        for i in range(3):
-            store_out(m, i).wait()
+    for i, h in enumerate((np_hbm, nqm_hbm, nqv_hbm)):
+        pltpu.make_async_copy(h, h, sem.at[i]).wait()
 
 
 def on_device(grads, param, q_m, m_scale, q_v, v_max, v_exp):
@@ -485,6 +488,7 @@
             pltpu.VMEM((N, 3, 4, c, LANES), f32),
             pltpu.VMEM((N, 3, c, LANES), f32),
             block(bf16), block(bf16),
+            pltpu.VMEM((3, N, 8, LANES), f32),
             pltpu.VMEM((16, LANES), f32),
             pltpu.VMEM((16, LANES), f32),
             pltpu.VMEM((8, LANES), f32),
@@ -517,7 +521,7 @@
         ),
         in_specs=[vmem] * 4,
         out_specs=(anywhere, anywhere, vmem, anywhere, vmem, vmem),
-        scratch_shapes=[block(bf16), block(bf16), pltpu.SemaphoreType.DMA((N, 3))],
+        scratch_shapes=[block(bf16), block(bf16), pltpu.SemaphoreType.DMA((3,))],
         compiler_params=pltpu.CompilerParams(vmem_limit_bytes=8 * 2**20),
     )(*kept)
     return new_param, new_q_m, ms[0], new_q_v, vm.T, ve.T

time: 164 us -> 163 us (level)
  no operation moved by 1% of the time
where the time goes in v4:
time: 163 us
  Pallas kernels  163 us (100%)
    pallas_call x1, Pallas kernels, on_device(): pl.pallas_call(kernel, out_shape=(block(f32), block(f32), block(f32), plt...  161 us

profile of v4, /device:TPU:1, one launch (start us, length us, event | category | flops | bytes accessed | tf_op | source)
XLA Modules:
  0.0 163.2 jit_solution(14206751395048396764)
XLA Ops:
  0.6 160.7 %shard_map.118 = (f32[8,256,128]{2,1,0:T(8,128)S(1)}, f32[8,256,128]{2,1,0:T(8,128)S(1)}, f32[8,256,128]{2,1,0:T(8,128)S(1)}, f32[1,128]{1,0:T(1,128)S(1)}) custom-call(bf16[4,4,4,2,256,256]{5,4,3,2,1,0:T(8,128)(2,1)} %bitcast.6, f32[4,256,256]{2,1,0:T(8,128)} %p_hbm.1, bf16[4,256,256]{2,1,0:T(8,128)(2,1)} %qm_hbm.1, f32[4]{0:T(128)} %ms_hbm.1, ...), custom_call_target="tpu_custom_call" | custom-call | tf_op jit(solution)/shard_map/pallas_call | solution.py:477
  161.3 1.9 %shard_map.119 = (f32[4,256,256]{2,1,0:T(8,128)}, bf16[4,256,256]{2,1,0:T(8,128)(2,1)}, f32[1,4]{1,0:T(1,128)}, bf16[4,256,256]{2,1,0:T(8,128)(2,1)}, f32[2,4]{1,0:T(2,128)}, /*index=5*/f32[2,4]{1,0:T(2,128)}) custom-call(f32[8,256,128]{2,1,0:T(8,128)S(1)} %get-tuple-element.16.par, f32[8,256,128]{2,1,0:T(8,128)S(1)} %get-tuple-element.17.mnew, ...), custom_call_target="tpu_custom_call" | custom-call | tf_op jit(solution)/shard_map/pallas_call | solution.py:512

commit v5 on v4

--- a/solution.py
+++ b/solution.py
@@ -17,8 +17,8 @@
 N = 8
 SEMS = 16
 LIMIT = 55 * 2**20
-ORDER = ('A1y', 'A2z', 'F2y', 'F2x', 'EC', 'EA', 'A1x', 'A3z', 'F2z', 'F1y', 'A2x', 'A2y', 'Z1a', 'F1x', 'Z1b', 'EB', 'S1')
-LAGS = {'S1': 0, 'A1y': 2, 'A1x': 2, 'Z1a': 3, 'Z1b': 4, 'F1y': 3, 'F1x': 3, 'A2z': 7, 'A2y': 4, 'A2x': 8, 'F2z': 20, 'F2y': 8, 'F2x': 22, 'A3z': 34, 'EA': 36, 'EB': 22, 'EC': 51}
+ORDER = ('F2x', 'EC', 'A1x', 'EA', 'A1y', 'A2z', 'F2z', 'F1y', 'F2y', 'Z1a', 'A2y', 'F1x', 'A2x', 'A3z', 'EB', 'Z1b', 'S1')
+LAGS = {'S1': 0, 'A1y': 2, 'A1x': 2, 'Z1a': 3, 'Z1b': 3, 'F1y': 3, 'F1x': 3, 'A2z': 7, 'A2y': 4, 'A2x': 6, 'F2z': 17, 'F2y': 8, 'F2x': 20, 'A3z': 24, 'EA': 28, 'EB': 20, 'EC': 33}
 
 
 def columns(ref, m):
@@ -424,7 +424,7 @@
             device_id=who[0], device_id_type=MESH,
         )
         everyone.wait_recv()
-        top = jnp.max(buf[...], axis=0, keepdims=True)
+        top = jnp.max(buf[0 : len(who) + 1], axis=0, keepdims=True)
         if phase == 0:
             stat[8:9] = top
         else:
@@ -489,9 +489,9 @@
             pltpu.VMEM((N, 3, c, LANES), f32),
             block(bf16), block(bf16),
             pltpu.VMEM((3, N, 8, LANES), f32),
+            pltpu.VMEM((24, LANES), f32),
+            pltpu.VMEM((32, LANES), f32),
             pltpu.VMEM((16, LANES), f32),
-            pltpu.VMEM((16, LANES), f32),
-            pltpu.VMEM((8, LANES), f32),
             pltpu.SMEM((4,), f32),
             pltpu.SMEM((2, 4), f32),
             pltpu.SMEM((2, 4), f32),

time: 163 us -> 163 us (level)
  no operation moved by 1% of the time
where the time goes in v5:
time: 163 us
  Pallas kernels  163 us (100%)
    pallas_call x1, Pallas kernels, on_device(): pl.pallas_call(kernel, out_shape=(block(f32), block(f32), block(f32), plt...  161 us

profile of v5, /device:TPU:1, one launch (start us, length us, event | category | flops | bytes accessed | tf_op | source)
XLA Modules:
  0.0 163.3 jit_solution(7010993644667189619)
XLA Ops:
  0.6 160.8 %shard_map.118 = (f32[8,256,128]{2,1,0:T(8,128)S(1)}, f32[8,256,128]{2,1,0:T(8,128)S(1)}, f32[8,256,128]{2,1,0:T(8,128)S(1)}, f32[1,128]{1,0:T(1,128)S(1)}) custom-call(bf16[4,4,4,2,256,256]{5,4,3,2,1,0:T(8,128)(2,1)} %bitcast.6, f32[4,256,256]{2,1,0:T(8,128)} %p_hbm.1, bf16[4,256,256]{2,1,0:T(8,128)(2,1)} %qm_hbm.1, f32[4]{0:T(128)} %ms_hbm.1, ...), custom_call_target="tpu_custom_call" | custom-call | tf_op jit(solution)/shard_map/pallas_call | solution.py:477
  161.5 1.9 %shard_map.119 = (f32[4,256,256]{2,1,0:T(8,128)}, bf16[4,256,256]{2,1,0:T(8,128)(2,1)}, f32[1,4]{1,0:T(1,128)}, bf16[4,256,256]{2,1,0:T(8,128)(2,1)}, f32[2,4]{1,0:T(2,128)}, /*index=5*/f32[2,4]{1,0:T(2,128)}) custom-call(f32[8,256,128]{2,1,0:T(8,128)S(1)} %get-tuple-element.16.par, f32[8,256,128]{2,1,0:T(8,128)S(1)} %get-tuple-element.17.mnew, ...), custom_call_target="tpu_custom_call" | custom-call | tf_op jit(solution)/shard_map/pallas_call | solution.py:512
